TPU v7x, 256 devices: a whole 4x4x8 slice. The times are simulated.
256 devices in a mesh: harm: 64 (over y, z, core), node: 4 (over x).
Axes of the slice: x: 4, y: 4, z: 8, core: 2. Of those that a mesh axis runs over, the one named last changes fastest.
Arguments:
- state: float32 [2, 128, 512, 128], P(None, 'harm', 'node'), may hold values from -0.6 to 0.6
- source: float32 [2, 128, 512, 128], P(None, 'harm', 'node'), may hold values from -6 to 6
- capacity: float32 [512, 128], P('node'), may hold values from 0.05 to 0.5
- row_shift: int32 [512], P('node'), may hold values from 0 to 3
- device_type: int32 [512, 128], P('node'), may hold values from 0 to 3
- device_table: float32 [3, 4], replicated, may hold values from 0.5 to 2
- precond: float32 [2, 128, 128, 128], P(None, 'harm'), may hold values from -1 to 1, as said below
Outputs:
- update: float32 [2, 128, 512, 128], P(None, 'harm', 'node')
- resid: float32 [2, 128, 512, 128], P(None, 'harm', 'node')
Inputs may be any that keep to these rules, and one draw needn't show every extreme that they name: precond[0, k] is 1/6 on the diagonal plus a full-rank fluctuation; precond[1, k] is a full-rank fluctuation.
All inputs are finite; a program needn't handle non-finite values.
Results may differ from a plain program's by a relative error of at most 0.00011.
Values sent between devices are 32-bit elements; how exact they have to be, the bound alone decides.
A program may use at most 64 MiB of HBM per device.

v0:
```python
import functools

import jax
import jax.numpy as jnp
from jax import lax
from jax.sharding import Mesh
from jax.sharding import PartitionSpec as P

ITERS = 3
TYPES = 4
SHIFTS = 4
HARM = ("harm_0", "harm_1", "harm_2")
HARM_NODE = ("harm_0", "harm_1", "harm_2", "node")


omega_step = 0.05
top = lax.Precision.HIGHEST


def extended(cells, sides, width):
    for axis, dim in sides:
        count = lax.axis_size(axis)
        ends = count - 1
        head = lax.slice_in_dim(cells, 0, width, axis=dim)
        tail = lax.slice_in_dim(cells, cells.shape[dim] - width, cells.shape[dim], axis=dim)
        cells = jnp.concatenate(
            [
                lax.ppermute(tail, axis, [(i, (i + 1) % count) for i in range(ends)]),
                cells,
                lax.ppermute(head, axis, [((i + 1) % count, i) for i in range(ends)]),
            ],
            axis=dim,
        )
    return cells


def by_axis(shard, axes):
    return functools.reduce(lax.psum, axes, shard)


def small_solve(gram, right):
    lower = jnp.linalg.cholesky(gram)
    order = gram.shape[0]
    forward = []
    for column in range(order):
        value = right[column]
        for member in range(column):
            value = value - lower[column, member] * forward[member]
        forward.append(value / lower[column, column])
    result = [None] * order
    for column in reversed(range(order)):
        value = forward[column]
        for member in range(column + 1, order):
            value = value - lower[member, column] * result[member]
        result[column] = value / lower[column, column]
    return result


def tables(harmonics, samples):
    waves = jnp.arange(harmonics, dtype=jnp.int32)
    moments = jnp.arange(samples, dtype=jnp.int32)
    phase = (moments[:, None] * waves[None, :] % samples).astype(jnp.float32) * (
        2.0 * jnp.pi / samples
    )
    cosine = jnp.cos(phase)
    sine = jnp.sin(phase)
    inverse = jnp.concatenate([cosine, -sine], axis=1)
    weights = jnp.where(waves == 0, 1.0, 2.0).astype(jnp.float32) / samples
    forward = jnp.concatenate([cosine.T * weights[:, None], -sine.T * weights[:, None]], axis=0)
    return (inverse, forward)


def stencil(field, above, below, capacity, shifts, waves):
    left_side = jnp.roll(field, 1, axis=3)
    right_side = jnp.roll(field, -1, axis=3)
    skewed = jnp.zeros_like(field)
    for amount in range(SHIFTS):
        picked = (shifts == amount).astype(jnp.float32)[None, None, :, None]
        skewed = skewed + picked * jnp.roll(above, -amount, axis=3)
    result = 4.0 * field - left_side - right_side - skewed - below
    reactive = omega_step * waves.astype(jnp.float32)[:, None, None] * capacity[None]
    return result + jnp.stack([-reactive * field[1], reactive * field[0]])


def precondition(field, blocks):
    real_part = jnp.einsum("krd,kcd->krc", field[0], blocks[0], precision=top) - jnp.einsum(
        "krd,kcd->krc", field[1], blocks[1], precision=top
    )
    imag_part = jnp.einsum("krd,kcd->krc", field[0], blocks[1], precision=top) + jnp.einsum(
        "krd,kcd->krc", field[1], blocks[0], precision=top
    )
    return jnp.stack([real_part, imag_part])


def body(state, source, capacity, row_shift, device_type, device_table, precond):
    groups = lax.axis_size(HARM)
    place = lax.axis_index(HARM)
    local_harm = state.shape[1]
    block_rows = state.shape[2]
    columns = state.shape[3]
    harmonics = local_harm * groups
    samples = 2 * harmonics
    own_rows = block_rows // groups
    inverse, forward = tables(harmonics, samples)
    kinds = lax.dynamic_slice_in_dim(device_type, place * own_rows, own_rows, 0).reshape(-1)
    params = jnp.zeros((3, kinds.shape[0]), jnp.float32)
    for member in range(TYPES):
        params = (
            params
            + (kinds == member).astype(jnp.float32)[None, :] * device_table[:, member][:, None]
        )
    linear, amplitude, slope = (params[0], params[1], params[2])

    def time_of(spectrum):
        return jnp.dot(
            inverse,
            spectrum.reshape(2 * harmonics, -1),
            precision=top,
            preferred_element_type=jnp.float32,
        )

    def spectrum_of(signal):
        return jnp.dot(forward, signal, precision=top, preferred_element_type=jnp.float32).reshape(
            2, harmonics, own_rows, columns
        )

    def currents(spectrum):
        voltage = time_of(spectrum)
        bent = jnp.tanh(slope * voltage)
        flow = linear * voltage + amplitude * bent
        slopes_now = linear + amplitude * slope * (1.0 - bent * bent)
        return (spectrum_of(flow), slopes_now)

    field_state, field_source = (state, source)
    waves = place * local_harm + jnp.arange(local_harm, dtype=jnp.int32)

    def sides(field):
        padded = extended(field, (("node", 2),), 1)
        return (padded[:, :, :-2], padded[:, :, 2:])

    def across(field, local):
        moved = lax.all_to_all(field, HARM, split_axis=2, concat_axis=1, tiled=True)
        result, extra = local(moved)
        return (lax.all_to_all(result, HARM, split_axis=1, concat_axis=2, tiled=True), extra)

    def operator(field):
        above, below = sides(field)
        return stencil(field, above, below, capacity, row_shift, waves)

    spec_flow, slopes = across(field_state, currents)
    resid = operator(field_state) + spec_flow - field_source

    def linear_part(spectrum):
        return (spectrum_of(slopes * time_of(spectrum)), slopes)

    start = -resid
    beta = jnp.sqrt(by_axis(jnp.sum(start * start), HARM_NODE))
    basis = [start / beta]
    directions = []
    columns_h = []
    for iteration in range(ITERS):
        direction = precondition(basis[iteration], precond)
        directions.append(direction)
        coupled, unused = across(direction, linear_part)
        image = operator(direction) + coupled
        locals_dot = jnp.stack([jnp.sum(basis[member] * image) for member in range(iteration + 1)])
        totals, square = (
            by_axis(locals_dot, HARM_NODE),
            by_axis(jnp.sum(image * image), HARM_NODE),
        )
        heights = [totals[member] for member in range(iteration + 1)]
        for earlier in range(iteration + 1):
            image = image - heights[earlier] * basis[earlier]
        length = jnp.sqrt(square - jnp.sum(totals * totals))
        columns_h.append(
            jnp.stack(heights + [length] + [jnp.zeros((), jnp.float32)] * (ITERS - 1 - iteration))
        )
        if iteration + 1 < ITERS:
            basis.append(image / length)
    hess = jnp.stack(columns_h, axis=1)
    gram = jnp.dot(hess.T, hess, precision=top)
    coeffs = small_solve(gram, beta * hess[0])
    update = jnp.zeros_like(field_state)
    for iteration in range(ITERS):
        update = update + coeffs[iteration] * directions[iteration]
    return (update, resid)


def solution(mesh):
    finer = Mesh(
        mesh.devices.reshape(4, 8, 2, mesh.shape["node"]), ("harm_0", "harm_1", "harm_2", "node")
    )
    return jax.shard_map(
        body,
        mesh=finer,
        in_specs=(
            P(None, HARM, "node", None),
            P(None, HARM, "node", None),
            P("node", None),
            P("node"),
            P("node", None),
            P(),
            P(None, HARM, None, None),
        ),
        out_specs=(P(None, HARM, "node", None), P(None, HARM, "node", None)),
        check_vma=False,
    )
```

profile of v0, /device:TPU:1, one launch (start us, length us, event | category | flops | bytes accessed | tf_op | source)
XLA Modules:
  0.0 375.9 jit_solution(4590156179275727498)
XLA Ops:
  1.4 3.9 %collective-permute-start = (f32[2,2,1,128]{3,2,1,0:T(1,128)S(1)}, f32[2,2,1,128]{3,2,1,0:T(1,128)S(1)}, u32[]{:S(2)}, u32[]{:S(2)}) collective-permute-start(f32[2,2,1,128]{3,2,1,0:T(1,128)S(1)} %get-tuple-element.69), channel_id=1, source_target_pairs={{0,1},{1,2},{2,3},{4,5},{5,6},{6,7},{8,9},{9,10},{10,11},{12,13},{... | collective-permute-start | bytes 6152 | tf_op jit(solution)/shard_map/ppermute | solution.py:28
  5.3 1.3 collective-permute-start.1
  6.6 1.9 copy.23
  8.5 12.7 %all-to-all-start = ((f32[2,2,128,128]{3,1,0,2:T(2,128)}), f32[2,2,128,128]{3,1,0,2:T(2,128)S(1)}, u32[]{:S(2)}, u32[]{:S(2)}) async-start(f32[2,2,128,128]{3,1,0,2:T(2,128)} %copy.23), calls=%async_computation | async-start | bytes 524288 | tf_op jit(solution)/shard_map/all_to_all | solution.py:142
  24.7 8.5 %all-to-all-done = f32[2,2,128,128]{3,1,0,2:T(2,128)S(1)} async-done(((f32[2,2,128,128]{3,1,0,2:T(2,128)}), f32[2,2,128,128]{3,1,0,2:T(2,128)S(1)}, u32[]{:S(2)}, u32[]{:S(2)}) %all-to-all-start) | async-done | bytes 262176 | tf_op jit(solution)/shard_map/all_to_all | solution.py:142
  35.1 6.0 %all-to-all-start.1 = ((f32[2,128,2,128]{3,2,0,1:T(2,128)}), f32[2,128,2,128]{3,2,0,1:T(2,128)S(1)}, u32[]{:S(2)}, u32[]{:S(2)}) async-start(f32[2,128,2,128]{3,2,0,1:T(2,128)} %copy.25), calls=%async_computation.1 | async-start | bytes 524288 | tf_op jit(solution)/shard_map/all_to_all | solution.py:144
  42.2 10.9 %all-to-all-done.1 = f32[2,128,2,128]{3,2,0,1:T(2,128)S(1)} async-done(((f32[2,128,2,128]{3,2,0,1:T(2,128)}), f32[2,128,2,128]{3,2,0,1:T(2,128)S(1)}, u32[]{:S(2)}, u32[]{:S(2)}) %all-to-all-start.1) | async-done | bytes 262176 | tf_op jit(solution)/shard_map/all_to_all | solution.py:144
  54.1 2.1 multiply_reduce_fusion.9
  56.2 9.0 %psum.196 = f32[]{:T(128)} all-reduce(f32[]{:T(128)} %get-tuple-element.41), channel_id=1, replica_groups=mesh['harm_0'=4,'harm_1'=8,'harm_2'=2,'node'=4] {'harm_0'}, use_global_device_ids=true, to_apply=%region_1.2 | all-reduce | flops 1 | bytes 8 | tf_op jit(solution)/shard_map/psum | solution.py:38
  65.1 11.8 %psum.197 = f32[]{:T(128)} all-reduce(f32[]{:T(128)} %psum.196), channel_id=1, replica_groups=mesh['harm_0'=4,'harm_1'=8,'harm_2'=2,'node'=4] {'harm_1'}, use_global_device_ids=true, to_apply=%region_2.3 | all-reduce | flops 1 | bytes 8 | tf_op jit(solution)/shard_map/psum | solution.py:38
  76.9 8.9 %psum.198 = f32[]{:T(128)} all-reduce(f32[]{:T(128)} %psum.197), channel_id=1, replica_groups=mesh['harm_0'=4,'harm_1'=8,'harm_2'=2,'node'=4] {'harm_2'}, use_global_device_ids=true, to_apply=%region_3.4 | all-reduce | flops 1 | bytes 8 | tf_op jit(solution)/shard_map/psum | solution.py:38
  85.8 10.2 %psum.199 = f32[]{:T(128)} all-reduce(f32[]{:T(128)} %psum.198), channel_id=1, replica_groups=mesh['harm_0'=4,'harm_1'=8,'harm_2'=2,'node'=4] {'node'}, use_global_device_ids=true, to_apply=%region_4.5 | all-reduce | flops 1 | bytes 8 | tf_op jit(solution)/shard_map/psum | solution.py:38
  100.2 7.5 %all-to-all-start.2 = ((f32[2,2,128,128]{3,1,0,2:T(2,128)}), f32[2,2,128,128]{3,1,0,2:T(2,128)S(1)}, u32[]{:S(2)}, u32[]{:S(2)}) async-start(f32[2,2,128,128]{3,1,0,2:T(2,128)} %copy.27), calls=%async_computation.2 | async-start | bytes 524288 | tf_op jit(solution)/shard_map/all_to_all | solution.py:142
  107.9 11.8 %all-to-all-done.2 = f32[2,2,128,128]{3,1,0,2:T(2,128)S(1)} async-done(((f32[2,2,128,128]{3,1,0,2:T(2,128)}), f32[2,2,128,128]{3,1,0,2:T(2,128)S(1)}, u32[]{:S(2)}, u32[]{:S(2)}) %all-to-all-start.2) | async-done | bytes 262176 | tf_op jit(solution)/shard_map/all_to_all | solution.py:142
  121.6 6.0 %all-to-all-start.3 = ((f32[2,128,2,128]{3,2,0,1:T(2,128)}), f32[2,128,2,128]{3,2,0,1:T(2,128)S(1)}, u32[]{:S(2)}, u32[]{:S(2)}) async-start(f32[2,128,2,128]{3,2,0,1:T(2,128)} %copy.29), calls=%async_computation.3 | async-start | bytes 524288 | tf_op jit(solution)/shard_map/all_to_all | solution.py:144
  127.6 1.3 collective-permute-start.2
  129.8 1.5 collective-permute-start.3
  135.4 4.2 %all-to-all-done.3 = f32[2,128,2,128]{3,2,0,1:T(2,128)S(1)} async-done(((f32[2,128,2,128]{3,2,0,1:T(2,128)}), f32[2,128,2,128]{3,2,0,1:T(2,128)S(1)}, u32[]{:S(2)}, u32[]{:S(2)}) %all-to-all-start.3) | async-done | bytes 262176 | tf_op jit(solution)/shard_map/all_to_all | solution.py:144
  140.8 2.3 multiply_reduce_fusion.8
  143.0 9.0 %all-reduce.8 = (f32[]{:T(128)}, f32[1]{0:T(128)}) all-reduce(f32[]{:T(128)} %get-tuple-element.10, f32[1]{0:T(128)} %bitcast.26), channel_id=1, replica_groups=mesh['harm_0'=4,'harm_1'=8,'harm_2'=2,'node'=4] {'harm_0'}, use_global_device_ids=true, to_apply=%region_11.12 | all-reduce | flops 2 | bytes 16 | tf_op jit(solution)/shard_map/psum | solution.py:38
  152.1 11.8 %all-reduce.2 = (f32[]{:T(128)}, f32[1]{0:T(128)}) all-reduce(f32[]{:T(128)} %get-tuple-element.31, f32[1]{0:T(128)} %get-tuple-element.32), channel_id=1, replica_groups=mesh['harm_0'=4,'harm_1'=8,'harm_2'=2,'node'=4] {'harm_1'}, use_global_device_ids=true, to_apply=%region_12.13 | all-reduce | flops 2 | bytes 16 | tf_op jit(solution)/shard_map/psum | solution.py:38
  163.8 9.0 %all-reduce.11 = (f32[]{:T(128)}, f32[1]{0:T(128)}) all-reduce(f32[]{:T(128)} %get-tuple-element.19, f32[1]{0:T(128)} %get-tuple-element.20), channel_id=1, replica_groups=mesh['harm_0'=4,'harm_1'=8,'harm_2'=2,'node'=4] {'harm_2'}, use_global_device_ids=true, to_apply=%region_13.14 | all-reduce | flops 2 | bytes 16 | tf_op jit(solution)/shard_map/psum | solution.py:38
  172.8 7.6 %all-reduce.5 = (f32[]{:T(128)}, f32[1]{0:T(128)}) all-reduce(f32[]{:T(128)} %get-tuple-element.37, f32[1]{0:T(128)} %get-tuple-element.38), channel_id=1, replica_groups=mesh['harm_0'=4,'harm_1'=8,'harm_2'=2,'node'=4] {'node'}, use_global_device_ids=true, to_apply=%region_14.15 | all-reduce | flops 2 | bytes 16 | tf_op jit(solution)/shard_map/psum | solution.py:38
  185.4 7.7 %all-to-all-start.4 = ((f32[2,2,128,128]{3,1,0,2:T(2,128)}), f32[2,2,128,128]{3,1,0,2:T(2,128)S(1)}, u32[]{:S(2)}, u32[]{:S(2)}) async-start(f32[2,2,128,128]{3,1,0,2:T(2,128)} %copy.32), calls=%async_computation.4 | async-start | bytes 524288 | tf_op jit(solution)/shard_map/all_to_all | solution.py:142
  193.3 11.8 %all-to-all-done.4 = f32[2,2,128,128]{3,1,0,2:T(2,128)S(1)} async-done(((f32[2,2,128,128]{3,1,0,2:T(2,128)}), f32[2,2,128,128]{3,1,0,2:T(2,128)S(1)}, u32[]{:S(2)}, u32[]{:S(2)}) %all-to-all-start.4) | async-done | bytes 262176 | tf_op jit(solution)/shard_map/all_to_all | solution.py:142
  206.9 6.2 %all-to-all-start.5 = ((f32[2,128,2,128]{3,2,0,1:T(2,128)}), f32[2,128,2,128]{3,2,0,1:T(2,128)}, u32[]{:S(2)}, u32[]{:S(2)}) async-start(f32[2,128,2,128]{3,2,0,1:T(2,128)} %copy.34), calls=%async_computation.5 | async-start | bytes 524288 | tf_op jit(solution)/shard_map/all_to_all | solution.py:144
  213.2 2.2 collective-permute-start.4
  216.4 1.3 collective-permute-start.5
  222.4 2.7 all-to-all-done.5
  227.1 3.0 multiply_reduce_fusion.6
  230.2 1.3 pad_maximum_fusion.22
  231.5 9.0 %all-reduce.7 = (f32[]{:T(128)}, f32[2]{0:T(128)S(1)}) all-reduce(f32[]{:T(128)} %get-tuple-element.7, f32[2]{0:T(128)S(1)} %pad_maximum_fusion.22), channel_id=1, replica_groups=mesh['harm_0'=4,'harm_1'=8,'harm_2'=2,'node'=4] {'harm_0'}, use_global_device_ids=true, to_apply=%region_22.23 | all-reduce | flops 3 | bytes 24 | tf_op jit(solution)/shard_map/psum | solution.py:38
  240.5 11.8 %all-reduce.1 = (f32[]{:T(128)}, f32[2]{0:T(128)S(1)}) all-reduce(f32[]{:T(128)} %get-tuple-element.29, f32[2]{0:T(128)S(1)} %get-tuple-element.30), channel_id=1, replica_groups=mesh['harm_0'=4,'harm_1'=8,'harm_2'=2,'node'=4] {'harm_1'}, use_global_device_ids=true, to_apply=%region_23.24 | all-reduce | flops 3 | bytes 24 | tf_op jit(solution)/shard_map/psum | solution.py:38
  252.2 9.0 %all-reduce.10 = (f32[]{:T(128)}, f32[2]{0:T(128)S(1)}) all-reduce(f32[]{:T(128)} %get-tuple-element.17, f32[2]{0:T(128)S(1)} %get-tuple-element.18), channel_id=1, replica_groups=mesh['harm_0'=4,'harm_1'=8,'harm_2'=2,'node'=4] {'harm_2'}, use_global_device_ids=true, to_apply=%region_24.25 | all-reduce | flops 3 | bytes 24 | tf_op jit(solution)/shard_map/psum | solution.py:38
  261.2 9.0 %all-reduce.4 = (f32[]{:T(128)}, f32[2]{0:T(128)S(1)}) all-reduce(f32[]{:T(128)} %get-tuple-element.35, f32[2]{0:T(128)S(1)} %get-tuple-element.36), channel_id=1, replica_groups=mesh['harm_0'=4,'harm_1'=8,'harm_2'=2,'node'=4] {'node'}, use_global_device_ids=true, to_apply=%region_25.26 | all-reduce | flops 3 | bytes 24 | tf_op jit(solution)/shard_map/psum | solution.py:38
  272.9 2.2 subtract_divide_fusion
  277.6 7.7 %all-to-all-start.6 = ((f32[2,2,128,128]{3,1,0,2:T(2,128)}), f32[2,2,128,128]{3,1,0,2:T(2,128)S(1)}, u32[]{:S(2)}, u32[]{:S(2)}) async-start(f32[2,2,128,128]{3,1,0,2:T(2,128)} %copy.37), calls=%async_computation.6 | async-start | bytes 524288 | tf_op jit(solution)/shard_map/all_to_all | solution.py:142
  287.5 9.8 %all-to-all-done.6 = f32[2,2,128,128]{3,1,0,2:T(2,128)S(1)} async-done(((f32[2,2,128,128]{3,1,0,2:T(2,128)}), f32[2,2,128,128]{3,1,0,2:T(2,128)S(1)}, u32[]{:S(2)}, u32[]{:S(2)}) %all-to-all-start.6) | async-done | bytes 262176 | tf_op jit(solution)/shard_map/all_to_all | solution.py:142
  299.1 6.2 %all-to-all-start.7 = ((f32[2,128,2,128]{3,2,0,1:T(2,128)}), f32[2,128,2,128]{3,2,0,1:T(2,128)}, u32[]{:S(2)}, u32[]{:S(2)}) async-start(f32[2,128,2,128]{3,2,0,1:T(2,128)} %copy.39), calls=%async_computation.7 | async-start | bytes 524288 | tf_op jit(solution)/shard_map/all_to_all | solution.py:144
  305.4 1.3 collective-permute-start.6
  306.7 1.3 collective-permute-start.7
  312.1 5.1 %all-to-all-done.7 = f32[2,128,2,128]{3,2,0,1:T(2,128)} async-done(((f32[2,128,2,128]{3,2,0,1:T(2,128)}), f32[2,128,2,128]{3,2,0,1:T(2,128)}, u32[]{:S(2)}, u32[]{:S(2)}) %all-to-all-start.7) | async-done | bytes 262176 | tf_op jit(solution)/shard_map/all_to_all | solution.py:144
  319.3 2.1 multiply_reduce_fusion.3
  321.5 1.9 pad_maximum_fusion.23
  323.4 9.0 %all-reduce.6 = (f32[]{:T(128)}, f32[3]{0:T(128)S(1)}) all-reduce(f32[]{:T(128)} %get-tuple-element.3, f32[3]{0:T(128)S(1)} %pad_maximum_fusion.23), channel_id=1, replica_groups=mesh['harm_0'=4,'harm_1'=8,'harm_2'=2,'node'=4] {'harm_0'}, use_global_device_ids=true, to_apply=%region_35.36 | all-reduce | flops 4 | bytes 32 | tf_op jit(solution)/shard_map/psum | solution.py:38
  332.3 11.8 %all-reduce = (f32[]{:T(128)}, f32[3]{0:T(128)S(1)}) all-reduce(f32[]{:T(128)} %get-tuple-element.27, f32[3]{0:T(128)S(1)} %get-tuple-element.28), channel_id=1, replica_groups=mesh['harm_0'=4,'harm_1'=8,'harm_2'=2,'node'=4] {'harm_1'}, use_global_device_ids=true, to_apply=%region_36.37 | all-reduce | flops 4 | bytes 32 | tf_op jit(solution)/shard_map/psum | solution.py:38
  344.1 8.9 %all-reduce.9 = (f32[]{:T(128)}, f32[3]{0:T(128)S(1)}) all-reduce(f32[]{:T(128)} %get-tuple-element.15, f32[3]{0:T(128)S(1)} %get-tuple-element.16), channel_id=1, replica_groups=mesh['harm_0'=4,'harm_1'=8,'harm_2'=2,'node'=4] {'harm_2'}, use_global_device_ids=true, to_apply=%region_37.38 | all-reduce | flops 4 | bytes 32 | tf_op jit(solution)/shard_map/psum | solution.py:38
  353.0 6.7 %all-reduce.3 = (f32[]{:T(128)}, f32[3]{0:T(128)S(1)}) all-reduce(f32[]{:T(128)} %get-tuple-element.33, f32[3]{0:T(128)S(1)} %get-tuple-element.34), channel_id=1, replica_groups=mesh['harm_0'=4,'harm_1'=8,'harm_2'=2,'node'=4] {'node'}, use_global_device_ids=true, to_apply=%region_38.39 | all-reduce | flops 4 | bytes 32 | tf_op jit(solution)/shard_map/psum | solution.py:38
  (169 shorter events, 51.3 us)
Async XLA Ops:
  1.4 23.1 %collective-permute-start = (f32[2,2,1,128]{3,2,1,0:T(1,128)S(1)}, f32[2,2,1,128]{3,2,1,0:T(1,128)S(1)}, u32[]{:S(2)}, u32[]{:S(2)}) collective-permute-start(f32[2,2,1,128]{3,2,1,0:T(1,128)S(1)} %get-tuple-element.69), channel_id=1, source_target_pairs={{0,1},{1,2},{2,3},{4,5},{5,6},{6,7},{8,9},{9,10},{10,11},{12,13},{... | collective-permute-start | bytes 6152 | tf_op jit(solution)/shard_map/ppermute | solution.py:28
  5.3 47.9 %collective-permute-start.1 = (f32[2,2,1,128]{3,2,1,0:T(1,128)S(1)}, f32[2,2,1,128]{3,2,1,0:T(1,128)S(1)}, u32[]{:S(2)}, u32[]{:S(2)}) collective-permute-start(f32[2,2,1,128]{3,2,1,0:T(1,128)S(1)} %get-tuple-element.70), channel_id=1, source_target_pairs={{1,0},{2,1},{3,2},{5,4},{6,5},{7,6},{9,8},{10,9},{11,10},{13,12},{... | collective-permute-start | bytes 6152 | tf_op jit(solution)/shard_map/ppermute | solution.py:30
  8.5 12.8 %copy-start.20 = (f32[3,4]{1,0:T(4,128)S(1)}, f32[3,4]{1,0:T(4,128)}, u32[]{:S(2)}) copy-start(f32[3,4]{1,0:T(4,128)} %param.12) | copy-start | bytes 148
  8.5 24.7 %all-to-all-start = ((f32[2,2,128,128]{3,1,0,2:T(2,128)}), f32[2,2,128,128]{3,1,0,2:T(2,128)S(1)}, u32[]{:S(2)}, u32[]{:S(2)}) async-start(f32[2,2,128,128]{3,1,0,2:T(2,128)} %copy.23), calls=%async_computation | async-start | bytes 524288 | tf_op jit(solution)/shard_map/all_to_all | solution.py:142
  21.2 1.6 copy-start
  22.3 0.8 copy-start.16
  23.1 0.8 copy-start.22
  35.1 18.0 %all-to-all-start.1 = ((f32[2,128,2,128]{3,2,0,1:T(2,128)}), f32[2,128,2,128]{3,2,0,1:T(2,128)S(1)}, u32[]{:S(2)}, u32[]{:S(2)}) async-start(f32[2,128,2,128]{3,2,0,1:T(2,128)} %copy.25), calls=%async_computation.1 | async-start | bytes 524288 | tf_op jit(solution)/shard_map/all_to_all | solution.py:144
  53.1 1.0 copy-start.15
  53.1 1.0 copy-start.17
  53.1 1.0 copy-start.18
  56.2 262.4 %copy-start.1 = (f32[2,2,128,128]{3,2,1,0:T(8,128)}, f32[2,2,128,128]{3,2,1,0:T(8,128)S(1)}, u32[]{:S(2)}) copy-start(f32[2,2,128,128]{3,2,1,0:T(8,128)S(1)} %get-tuple-element.42) | copy-start | bytes 786436
  96.7 1.0 copy-start.2
  100.2 19.5 %all-to-all-start.2 = ((f32[2,2,128,128]{3,1,0,2:T(2,128)}), f32[2,2,128,128]{3,1,0,2:T(2,128)S(1)}, u32[]{:S(2)}, u32[]{:S(2)}) async-start(f32[2,2,128,128]{3,1,0,2:T(2,128)} %copy.27), calls=%async_computation.2 | async-start | bytes 524288 | tf_op jit(solution)/shard_map/all_to_all | solution.py:142
  121.6 18.0 %all-to-all-start.3 = ((f32[2,128,2,128]{3,2,0,1:T(2,128)}), f32[2,128,2,128]{3,2,0,1:T(2,128)S(1)}, u32[]{:S(2)}, u32[]{:S(2)}) async-start(f32[2,128,2,128]{3,2,0,1:T(2,128)} %copy.29), calls=%async_computation.3 | async-start | bytes 524288 | tf_op jit(solution)/shard_map/all_to_all | solution.py:144
  127.6 3.7 collective-permute-start.2
  129.8 10.0 %collective-permute-start.3 = (f32[2,2,1,128]{3,2,1,0:T(1,128)S(1)}, f32[2,2,1,128]{3,2,1,0:T(1,128)S(1)}, u32[]{:S(2)}, u32[]{:S(2)}) collective-permute-start(f32[2,2,1,128]{3,2,1,0:T(1,128)S(1)} %get-tuple-element.62), channel_id=1, source_target_pairs={{1,0},{2,1},{3,2},{5,4},{6,5},{7,6},{9,8},{10,9},{11,10},{13,12},{... | collective-permute-start | bytes 6152 | tf_op jit(solution)/shard_map/ppermute | solution.py:30
  139.6 1.0 copy-start.13
  139.6 1.0 copy-start.14
  139.6 1.1 copy-start.11
  139.6 1.2 copy-start.12
  185.4 19.7 %all-to-all-start.4 = ((f32[2,2,128,128]{3,1,0,2:T(2,128)}), f32[2,2,128,128]{3,1,0,2:T(2,128)S(1)}, u32[]{:S(2)}, u32[]{:S(2)}) async-start(f32[2,2,128,128]{3,1,0,2:T(2,128)} %copy.32), calls=%async_computation.4 | async-start | bytes 524288 | tf_op jit(solution)/shard_map/all_to_all | solution.py:142
  206.9 18.1 %all-to-all-start.5 = ((f32[2,128,2,128]{3,2,0,1:T(2,128)}), f32[2,128,2,128]{3,2,0,1:T(2,128)}, u32[]{:S(2)}, u32[]{:S(2)}) async-start(f32[2,128,2,128]{3,2,0,1:T(2,128)} %copy.34), calls=%async_computation.5 | async-start | bytes 524288 | tf_op jit(solution)/shard_map/all_to_all | solution.py:144
  213.2 4.5 %collective-permute-start.4 = (f32[2,2,1,128]{3,2,1,0:T(1,128)S(1)}, f32[2,2,1,128]{3,2,1,0:T(1,128)S(1)}, u32[]{:S(2)}, u32[]{:S(2)}) collective-permute-start(f32[2,2,1,128]{3,2,1,0:T(1,128)S(1)} %get-tuple-element.55), channel_id=1, source_target_pairs={{0,1},{1,2},{2,3},{4,5},{5,6},{6,7},{8,9},{9,10},{10,11},{12,13},{... | collective-permute-start | bytes 6152 | tf_op jit(solution)/shard_map/ppermute | solution.py:28
  216.4 10.0 %collective-permute-start.5 = (f32[2,2,1,128]{3,2,1,0:T(1,128)S(1)}, f32[2,2,1,128]{3,2,1,0:T(1,128)S(1)}, u32[]{:S(2)}, u32[]{:S(2)}) collective-permute-start(f32[2,2,1,128]{3,2,1,0:T(1,128)S(1)} %get-tuple-element.56), channel_id=1, source_target_pairs={{1,0},{2,1},{3,2},{5,4},{6,5},{7,6},{9,8},{10,9},{11,10},{13,12},{... | collective-permute-start | bytes 6152 | tf_op jit(solution)/shard_map/ppermute | solution.py:30
  225.1 1.3 copy-start.9
  225.1 1.3 copy-start.10
  226.1 1.0 copy-start.7
  226.1 1.0 copy-start.8
  277.6 19.7 %all-to-all-start.6 = ((f32[2,2,128,128]{3,1,0,2:T(2,128)}), f32[2,2,128,128]{3,1,0,2:T(2,128)S(1)}, u32[]{:S(2)}, u32[]{:S(2)}) async-start(f32[2,2,128,128]{3,1,0,2:T(2,128)} %copy.37), calls=%async_computation.6 | async-start | bytes 524288 | tf_op jit(solution)/shard_map/all_to_all | solution.py:142
  299.1 18.1 %all-to-all-start.7 = ((f32[2,128,2,128]{3,2,0,1:T(2,128)}), f32[2,128,2,128]{3,2,0,1:T(2,128)}, u32[]{:S(2)}, u32[]{:S(2)}) async-start(f32[2,128,2,128]{3,2,0,1:T(2,128)} %copy.39), calls=%async_computation.7 | async-start | bytes 524288 | tf_op jit(solution)/shard_map/all_to_all | solution.py:144
  305.4 3.4 collective-permute-start.6
  306.7 11.8 %collective-permute-start.7 = (f32[2,2,1,128]{3,2,1,0:T(1,128)S(1)}, f32[2,2,1,128]{3,2,1,0:T(1,128)S(1)}, u32[]{:S(2)}, u32[]{:S(2)}) collective-permute-start(f32[2,2,1,128]{3,2,1,0:T(1,128)S(1)} %get-tuple-element.50), channel_id=1, source_target_pairs={{1,0},{2,1},{3,2},{5,4},{6,5},{7,6},{9,8},{10,9},{11,10},{13,12},{... | collective-permute-start | bytes 6152 | tf_op jit(solution)/shard_map/ppermute | solution.py:30
  311.3 7.2 %copy-start.19 = (f32[1,2,128,128]{3,2,1,0:T(8,128)S(1)}, f32[1,2,128,128]{3,2,1,0:T(8,128)}, u32[]{:S(2)}) copy-start(f32[1,2,128,128]{3,2,1,0:T(8,128)} %get-tuple-element.72) | copy-start | bytes 393220
  317.3 1.3 copy-start.5
  317.3 1.3 copy-start.6
  318.3 1.0 copy-start.3
  318.3 1.0 copy-start.4
  361.8 0.6 copy-start.21
where the time goes:
time: 379 us; the launch traced here: 376 us
  blocking collectives  152 us (40%)
  starting transfers between devices  74.3 us (20%)
  waiting for transfers between devices  64.8 us (17%)
  local copies, waits for them, and re-layouts  31.7 us (8%)
  other arithmetic  28.6 us (8%)
  between operations  16.3 us (4%)
  matrix products  7.84 us (2%)
    psum x16, blocking collectives, by_axis(): return functools.reduce(lax.psum, axes, shard)  152 us
    all_to_all x4, waiting for transfers between devices, across(): moved = lax.all_to_all(field, HARM, split_axis=2, concat_axis=1, tiled=True)  41.9 us
    all_to_all x4, starting transfers between devices, across(): moved = lax.all_to_all(field, HARM, split_axis=2, concat_axis=1, tiled=True)  35.7 us
    all_to_all x4, starting transfers between devices, across(): lax.all_to_all(result, HARM, split_axis=1, concat_axis=2, tiled=True)  24.5 us
    all_to_all x4, waiting for transfers between devices, across(): lax.all_to_all(result, HARM, split_axis=1, concat_axis=2, tiled=True)  22.9 us
    slice x18, local copies, waits for them, and re-layouts, stencil(): skewed = skewed + picked * jnp.roll(above, -amount, axis=3)  12 us
    ppermute x4, starting transfers between devices, extended(): lax.ppermute(tail, axis, [(i, (i + 1) % count) for i in range(ends)])  8.73 us
  transfers between devices with their start and end apart: 16, of which 8 were waited for; matrix products, arithmetic and copies ran while one was open for 7% of the time, Pallas kernels for 0%

commit v1 on v0

v1 whole, which is shorter than its diff:
```python
import functools

import jax
import jax.numpy as jnp
import numpy as np
from jax import lax
from jax.experimental import pallas as pl
from jax.experimental.pallas import tpu as pltpu
from jax.sharding import PartitionSpec as P

ITERS = 3
TYPES = 4
SHIFTS = 4
OMEGA = 0.05
MESH = pl.DeviceIdType.MESH
F32 = jnp.float32
BF16 = jnp.bfloat16


def split(x):
    high = x.astype(BF16)
    low = (x - high.astype(F32)).astype(BF16)
    return high, low


def tables(harmonics):
    samples = 2 * harmonics
    row = np.arange(2 * harmonics)
    wave = (row // 4) * 2 + row % 2
    part = (row // 2) % 2
    moment = np.arange(samples)
    phase = (moment[:, None] * wave[None, :] % samples) * (2.0 * np.pi / samples)
    inverse = np.where(part[None, :] == 0, np.cos(phase), -np.sin(phase))
    weight = np.where(wave == 0, 1.0, 2.0) / samples
    forward = inverse.T * weight[:, None]

    def stacked(matrix):
        matrix = matrix.astype(np.float32)
        high = matrix.astype(jnp.bfloat16)
        low = (matrix - high.astype(np.float32)).astype(jnp.bfloat16)
        return np.concatenate([high, low, high], axis=1)

    return stacked(inverse), stacked(forward)


def kernel(
    state_hbm, source_hbm, cap_hbm, shift_hbm, kinds_hbm, table, precond_hbm, inv_hbm, fwd_hbm,
    update_hbm, resid_hbm,
    state, source, cap, shift, kinds, precond, inv, fwd,
    weights, slopes, basis, images, directions, out_update, out_resid,
    t_send, t_recv, l_send, l_recv, halo_send, halo_recv, ar_send, ar_recv, ax_send, ax_recv,
    in_sem, out_sem, t_ssem, t_rsem, l_ssem, l_rsem, h_ssem, h_rsem, a_ssem, a_rsem, x_ssem, x_rsem,
):
    harm = lax.axis_index("harm")
    node = lax.axis_index("node")
    y, z, core = harm // 16, lax.rem(harm // 2, 8), lax.rem(harm, 2)
    inputs = [
        (state_hbm, state), (inv_hbm, inv), (kinds_hbm, kinds), (fwd_hbm, fwd),
        (precond_hbm, precond), (shift_hbm, shift), (cap_hbm, cap), (source_hbm, source),
    ]
    loads = [pltpu.make_async_copy(a, b, in_sem.at[i]) for i, (a, b) in enumerate(inputs)]
    for load in loads:
        load.start()

    def peer(j):
        i, jy, jc = j // 8, lax.rem(j // 2, 4), lax.rem(j, 2)
        dz = jnp.where(lax.rem(i, 2) == 0, 4 + i // 2, 4 - (i + 1) // 2)
        dy = jnp.where(lax.rem(jy, 2) == 0, 2 + jy // 2, 2 - (jy + 1) // 2)
        dc = 1 - jc
        return lax.rem(y + dy, 4) * 16 + lax.rem(z + dz, 8) * 2 + lax.rem(core + dc, 2)

    barrier = pltpu.get_barrier_semaphore()

    @pl.loop(0, 63)
    def _(j):
        pl.semaphore_signal(barrier, inc=1, device_id=(peer(j), node), device_id_type=MESH)

    for d in (1, 2, 3):
        pl.semaphore_signal(
            barrier, inc=1, device_id=(harm, lax.rem(node + d, 4)), device_id_type=MESH
        )

    def tile(index):
        return pl.ds(pl.multiple_of(index * 8, 8), 8)

    def exchange(send, recv, ssem, rsem, stage):
        @pl.loop(0, 63)
        def _(j):
            other = peer(j)
            pltpu.make_async_remote_copy(
                src_ref=send.at[stage, tile(other)],
                dst_ref=recv.at[stage, tile(harm)],
                send_sem=ssem.at[stage],
                recv_sem=rsem.at[stage],
                device_id=(other, node),
                device_id_type=MESH,
            ).start()

        recv[stage, tile(harm), :] = send[stage, tile(harm), :]

    def arrived(send, recv, ssem, rsem, stage):
        return pltpu.make_async_remote_copy(
            src_ref=send.at[stage, pl.ds(0, 504)],
            dst_ref=recv.at[stage, pl.ds(0, 504)],
            send_sem=ssem.at[stage],
            recv_sem=rsem.at[stage],
            device_id=(lax.rem(harm + 1, 64), node),
            device_id_type=MESH,
        )

    t_all = (t_send, t_recv, t_ssem, t_rsem)
    l_all = (l_send, l_recv, l_ssem, l_rsem)

    def halo_copy(stage, side):
        step = 1 if side == 0 else 3
        return pltpu.make_async_remote_copy(
            src_ref=halo_send.at[stage, side],
            dst_ref=halo_recv.at[stage, side],
            send_sem=h_ssem.at[stage, side],
            recv_sem=h_rsem.at[stage, side],
            device_id=(harm, lax.rem(node + step, 4)),
            device_id_type=MESH,
        )

    pairs = [(p, kk) for p in range(2) for kk in range(2)]

    def to_time(field, stage):
        for p, kk in pairs:
            for i in range(2):
                q = (p * 2 + kk) * 2 + i
                t_send[stage, pl.ds(q, 64, stride=8), :] = field[p, kk, i * 64 : (i + 1) * 64, :]
        last = [field[p, kk, 127:128, :] for p, kk in pairs]
        first = [field[p, kk, 0:1, :] for p, kk in pairs]
        halo_send[stage, 0] = jnp.concatenate(last + last, axis=0)
        halo_send[stage, 1] = jnp.concatenate(first + first, axis=0)

    def depart(stage):
        exchange(*t_all, stage)
        for side in range(2):
            halo_copy(stage, side).start()

    def rhs(x):
        high, low = split(x)
        return jnp.concatenate([high, high, low], axis=0)

    def time_of(stage):
        u = jnp.concatenate(
            [t_recv[stage, pl.ds(i, 256, stride=2), :] for i in range(2)], axis=1
        )
        return jnp.dot(inv[...], rhs(u), preferred_element_type=F32)

    def to_spec(signal, stage):
        spec = jnp.dot(fwd[...], rhs(signal), preferred_element_type=F32)
        for i in range(2):
            l_send[stage, pl.ds(i, 256, stride=2), :] = spec[:, i * 128 : (i + 1) * 128]
        exchange(*l_all, stage)

    def spec_part(stage, p, kk):
        q = (p * 2 + kk) * 2
        return jnp.concatenate(
            [l_recv[stage, pl.ds(q + i, 64, stride=8), :] for i in range(2)], axis=0
        )

    loads[0].wait()
    to_time(state, 0)
    pl.semaphore_wait(barrier, 66)
    depart(0)

    for load in loads[1:]:
        load.wait()
    for kk in range(2):
        real, imag = precond[0, kk].T, precond[1, kk].T
        whole = jnp.concatenate(
            [jnp.concatenate([real, imag], axis=1), jnp.concatenate([-imag, real], axis=1)], axis=0
        )
        high, low = split(whole)
        weights[kk, 0:256, :] = high
        weights[kk, 256:512, :] = high
        weights[kk, 512:768, :] = low
    kind = jnp.concatenate([kinds[pl.ds(harm, 1), :], kinds[pl.ds(harm + 64, 1), :]], axis=1)
    linear, amplitude, slope = [
        sum(jnp.where(kind == member, table[what, member], 0.0) for member in range(TYPES))
        for what in range(3)
    ]
    shifts = jnp.broadcast_to(shift[...].astype(F32), (128, 128)).T
    row = lax.broadcasted_iota(jnp.int32, (128, 128), 0)
    waves = [(2 * harm + kk).astype(F32) * OMEGA for kk in range(2)]
    not_first = jnp.where(node == 0, 0.0, 1.0)
    not_last = jnp.where(node == 3, 0.0, 1.0)

    def stencil(field, stage, p, kk):
        f = field[p, kk]
        index = p * 2 + kk
        halo_a = halo_recv[stage, 0, index : index + 1, :] * not_first
        halo_b = halo_recv[stage, 1, index : index + 1, :] * not_last
        above = jnp.where(row == 0, halo_a, pltpu.roll(f, 1, axis=0))
        below = jnp.where(row == 127, halo_b, pltpu.roll(f, 127, axis=0))
        skewed = above
        for amount in range(1, SHIFTS):
            skewed = jnp.where(
                shifts == float(amount), pltpu.roll(above, 128 - amount, axis=1), skewed
            )
        sides = pltpu.roll(f, 1, axis=1) + pltpu.roll(f, 127, axis=1)
        result = 4.0 * f - sides - skewed - below
        turned = waves[kk] * cap[...] * field[1 - p, kk]
        return result - turned if p == 0 else result + turned

    def halo_wait(stage):
        for side in range(2):
            halo_copy(stage, side).wait_recv()

    def precondition(field, target):
        for kk in range(2):
            high, low = split(jnp.concatenate([field[0, kk], field[1, kk]], axis=1))
            both = jnp.dot(
                jnp.concatenate([high, low, high], axis=1),
                weights[kk],
                preferred_element_type=F32,
            )
            target[0, kk] = both[:, 0:128]
            target[1, kk] = both[:, 128:256]

    lane = lax.broadcasted_iota(jnp.int32, (1, 128), 1)

    def inner(a, b):
        total = sum(a[p, kk] * b[p, kk] for p, kk in pairs)
        return jnp.sum(jnp.sum(total, axis=0, keepdims=True), axis=1, keepdims=True)

    def reduce_start(stage, values):
        packed = sum(jnp.where(lane == q, value, 0.0) for q, value in enumerate(values))
        ar_send[stage] = packed

        @pl.loop(0, 63)
        def _(j):
            pltpu.make_async_remote_copy(
                src_ref=ar_send.at[stage],
                dst_ref=ar_recv.at[stage, harm],
                send_sem=a_ssem.at[stage],
                recv_sem=a_rsem.at[stage],
                device_id=(peer(j), node),
                device_id_type=MESH,
            ).start()

        ar_recv[stage, harm] = packed

    def reduce_all(stage):
        return pltpu.make_async_remote_copy(
            src_ref=ar_recv.at[stage, pl.ds(0, 63)],
            dst_ref=ar_recv.at[stage, pl.ds(0, 63)],
            send_sem=a_ssem.at[stage],
            recv_sem=a_rsem.at[stage],
            device_id=(lax.rem(harm + 1, 64), node),
            device_id_type=MESH,
        )

    def ax_copy(stage, d):
        return pltpu.make_async_remote_copy(
            src_ref=ax_send.at[stage],
            dst_ref=ax_recv.at[stage, node],
            send_sem=x_ssem.at[stage, d],
            recv_sem=x_rsem.at[stage, d],
            device_id=(harm, lax.rem(node + d + 1, 4)),
            device_id_type=MESH,
        )

    def reduce_middle(stage):
        reduce_all(stage).wait_recv()
        total = jnp.sum(ar_recv[stage], axis=0)
        ax_send[stage] = total
        for d in range(3):
            ax_copy(stage, d).start()
        ax_recv[stage, node] = total

    def reduce_finish(stage):
        for d in range(3):
            ax_copy(stage, d).wait_recv()
        total = jnp.sum(ax_recv[stage], axis=0)
        return lambda q: total[:, q : q + 1]

    arrived(*t_all, 0).wait_recv()
    voltage = time_of(0)
    bent = jnp.tanh(slope * voltage)
    slopes[...] = linear + amplitude * slope * (1.0 - bent * bent)
    to_spec(linear * voltage + amplitude * bent, 0)
    halo_wait(0)
    p0, p1 = basis.at[0], basis.at[1]
    for p, kk in pairs:
        basis[0, p, kk] = source[p, kk] - stencil(state, 0, p, kk)
    arrived(*l_all, 0).wait_recv()
    for p, kk in pairs:
        start = basis[0, p, kk] - spec_part(0, p, kk)
        basis[0, p, kk] = start
        out_resid[p, kk] = -start
    resid_out = pltpu.make_async_copy(out_resid, resid_hbm, out_sem.at[0])
    resid_out.start()

    def send_direction(source_ref, stage):
        precondition(source_ref, directions.at[stage - 1])
        to_time(directions.at[stage - 1], stage)
        depart(stage)

    def apply_time(stage):
        arrived(*t_all, stage).wait_recv()
        to_spec(slopes[...] * time_of(stage), stage)

    def local_image(stage):
        halo_wait(stage)
        for p, kk in pairs:
            images[stage - 1, p, kk] = stencil(directions.at[stage - 1], stage, p, kk)

    send_direction(p0, 1)
    apply_time(1)
    local_image(1)
    arrived(*l_all, 1).wait_recv()
    for p, kk in pairs:
        images[0, p, kk] = images[0, p, kk] + spec_part(1, p, kk)
    z0, z1, z2 = [directions.at[j] for j in range(3)]
    i0, i1, i2 = [images.at[j] for j in range(3)]

    send_direction(i0, 2)
    reduce_start(0, [inner(p0, p0), inner(p0, i0), inner(i0, i0)])
    apply_time(2)
    local_image(2)
    reduce_middle(0)
    first = reduce_finish(0)
    h = first(1) / first(0)
    for p, kk in pairs:
        basis[1, p, kk] = i0[p, kk] - h * p0[p, kk]
        directions[1, p, kk] = z1[p, kk] - h * z0[p, kk]
        images[1, p, kk] = i1[p, kk] - h * i0[p, kk]
    arrived(*l_all, 2).wait_recv()
    for p, kk in pairs:
        images[1, p, kk] = images[1, p, kk] + spec_part(2, p, kk)

    send_direction(i1, 3)
    reduce_start(
        1, [inner(p0, i1), inner(p1, i1), inner(p1, p1), inner(i0, i1), inner(i1, i1)]
    )
    apply_time(3)
    local_image(3)
    reduce_middle(1)
    second = reduce_finish(1)
    h0, h1 = second(0) / first(0), second(1) / second(2)
    for p, kk in pairs:
        directions[2, p, kk] = z2[p, kk] - h0 * z0[p, kk] - h1 * z1[p, kk]
        images[2, p, kk] = i2[p, kk] - h0 * i0[p, kk] - h1 * i1[p, kk]
    arrived(*l_all, 3).wait_recv()
    for p, kk in pairs:
        images[2, p, kk] = images[2, p, kk] + spec_part(3, p, kk)
    reduce_start(2, [inner(p0, i2), inner(i0, i2), inner(i1, i2), inner(i2, i2)])
    reduce_middle(2)
    third = reduce_finish(2)

    g00, g01, g02 = first(2), second(3), third(1)
    g11, g12, g22 = second(4), third(2), third(3)
    b0, b1, b2 = first(1), second(0), third(0)
    l10, l20 = g01 / g00, g02 / g00
    d1 = g11 - l10 * g01
    e12 = g12 - l10 * g02
    c1 = b1 - l10 * b0
    l21 = e12 / d1
    d2 = g22 - l20 * g02 - l21 * e12
    c2 = b2 - l20 * b0 - l21 * c1
    y2 = c2 / d2
    y1 = (c1 - e12 * y2) / d1
    y0 = (b0 - g01 * y1 - g02 * y2) / g00
    for p, kk in pairs:
        out_update[p, kk] = y0 * z0[p, kk] + y1 * z1[p, kk] + y2 * z2[p, kk]
    update_out = pltpu.make_async_copy(out_update, update_hbm, out_sem.at[1])
    update_out.start()

    for stage in range(4):
        arrived(*t_all, stage).wait_send()
        arrived(*l_all, stage).wait_send()
        for side in range(2):
            halo_copy(stage, side).wait_send()
    for stage in range(3):
        reduce_all(stage).wait_send()
        for d in range(3):
            ax_copy(stage, d).wait_send()
    resid_out.wait()
    update_out.wait()


def body(state, source, capacity, row_shift, device_type, device_table, precond):
    inverse, forward = tables(state.shape[1] * lax.axis_size("harm"))
    block = (2, 2, 128, 128)
    vmem = pltpu.VMEM
    dma = pltpu.SemaphoreType.DMA
    hbm = pl.BlockSpec(memory_space=pl.ANY)
    update, resid = pl.pallas_call(
        kernel,
        out_shape=[jax.ShapeDtypeStruct(block, F32)] * 2,
        in_specs=[hbm] * 5 + [pl.BlockSpec(memory_space=pltpu.SMEM)] + [hbm] * 3,
        out_specs=[hbm, hbm],
        scratch_shapes=[
            vmem(block, F32), vmem(block, F32), vmem((128, 128), F32), vmem((1, 128), jnp.int32),
            vmem((128, 128), jnp.int32), vmem(block, F32), vmem((256, 768), BF16),
            vmem((256, 768), BF16),
            vmem((2, 768, 256), BF16), vmem((256, 256), F32), vmem((2,) + block, F32),
            vmem((3,) + block, F32), vmem((3,) + block, F32), vmem(block, F32), vmem(block, F32),
            vmem((4, 512, 128), F32), vmem((4, 512, 128), F32),
            vmem((4, 512, 128), F32), vmem((4, 512, 128), F32),
            vmem((4, 2, 8, 128), F32), vmem((4, 2, 8, 128), F32),
            vmem((3, 1, 128), F32), vmem((3, 64, 1, 128), F32),
            vmem((3, 1, 128), F32), vmem((3, 4, 1, 128), F32),
            dma((8,)), dma((2,)), dma((4,)), dma((4,)), dma((4,)), dma((4,)),
            dma((4, 2)), dma((4, 2)), dma((3,)), dma((3,)), dma((3, 3)), dma((3, 3)),
        ],
        compiler_params=pltpu.CompilerParams(
            collective_id=0, has_side_effects=True, vmem_limit_bytes=40 * 2**20
        ),
    )(
        state, source, capacity, row_shift.reshape(1, -1), device_type, device_table, precond,
        jnp.asarray(inverse), jnp.asarray(forward),
    )
    return update, resid


def solution(mesh):
    harm, node = mesh.axis_names
    return jax.shard_map(
        body,
        mesh=mesh,
        in_specs=(
            P(None, harm, node, None),
            P(None, harm, node, None),
            P(node, None),
            P(node),
            P(node, None),
            P(),
            P(None, harm, None, None),
        ),
        out_specs=(P(None, harm, node, None), P(None, harm, node, None)),
        check_vma=False,
    )
```

time: 379 us -> 112 us (0.30)
  blocking collectives: 152 us -> 0 us
  Pallas kernels: 0 us -> 101 us
  starting transfers between devices: 74.3 us -> 0 us
  waiting for transfers between devices: 64.8 us -> 0 us
  other arithmetic: 28.6 us -> 0 us
  local copies, waits for them, and re-layouts: 31.7 us -> 9.25 us
  between operations: 16.3 us -> 0.66 us
  matrix products: 7.84 us -> 0 us
    psum x16 -> x0, blocking collectives: 152 us -> none  [by_axis(): return functools.reduce(lax.psum, axes, shard)]
    pallas_call x0 -> x1, Pallas kernels: none -> 101 us  [body(): pl.pallas_call(kernel, out_shape=[jax.ShapeDtypeStruct(block, F32)] * 2,...]
    all_to_all x8 -> x0, waiting for transfers between devices: 64.8 us -> none  [the longest x4 41.9 us: across(): moved = lax.all_to_all(field, HARM, split_axis=2, concat_axis=1, tiled=True)]
    all_to_all x8 -> x0, starting transfers between devices: 60.2 us -> none  [the longest x4 35.7 us: across(): moved = lax.all_to_all(field, HARM, split_axis=2, concat_axis=1, tiled=True)]
    slice x23 -> x0, local copies, waits for them, and re-layouts: 14.8 us -> none  [the longest x18 12 us: stencil(): skewed = skewed + picked * jnp.roll(above, -amount, axis=3)]
    ppermute x8 -> x0, starting transfers between devices: 14.1 us -> none  [the longest x4 8.73 us: extended(): lax.ppermute(tail, axis, [(i, (i + 1) % count) for i in range(ends)])]
    reduce_sum x6 -> x0, other arithmetic: 10.8 us -> none  [the longest x3 7.47 us: body(): jnp.sum(basis[member] * image)]
    another operation x24 -> x0, other arithmetic: 9.43 us -> none  [the longest x2 3.19 us: body(): jnp.stack([jnp.sum(basis[member] * image) for member in range(iteration +...]
  transfers between devices with their start and end apart: 16 -> 0, of which waited for: 8 -> 0; matrix products, arithmetic and copies ran while one was open for 7% -> 0% of each run, Pallas kernels for 0% -> 0%
where the time goes in v1:
time: 112 us; the launch traced here: 111 us
  Pallas kernels  101 us (90%)
  local copies, waits for them, and re-layouts  9.25 us (8%)
    pallas_call x1, Pallas kernels, body(): pl.pallas_call(kernel, out_shape=[jax.ShapeDtypeStruct(block, F32)] * 2,...  101 us
    unnamed x20, local copies, waits for them, and re-layouts  9.25 us

profile of v1, /device:TPU:1, one launch (start us, length us, event | category | flops | bytes accessed | tf_op | source)
XLA Modules:
  0.0 111.3 jit_solution(7169601761192066312)
XLA Ops:
  0.6 0.0 copy-start.8
  0.6 0.6 copy-done.8
  1.3 0.0 copy-start
  1.3 1.0 copy-done
  2.3 0.0 copy-start.1
  2.3 1.0 copy-done.1
  3.3 0.0 copy-start.2
  3.3 0.9 copy-done.2
  4.2 0.0 copy-start.3
  4.2 0.9 copy-done.3
  5.2 0.0 copy-start.4
  5.2 0.9 copy-done.4
  6.1 0.0 copy-start.5
  6.1 0.8 copy-done.5
  7.0 0.0 copy-start.6
  7.0 0.8 copy-done.6
  7.8 0.0 copy-start.7
  7.8 0.7 copy-done.7
  8.5 101.4 %shard_map.104 = (f32[2,2,128,128]{3,2,1,0:T(8,128)S(1)}, f32[2,2,128,128]{3,2,1,0:T(8,128)S(1)}) custom-call(f32[2,2,128,128]{3,2,1,0:T(8,128)S(1)} %copy-done.2, f32[2,2,128,128]{3,2,1,0:T(8,128)S(1)} %copy-done.3, f32[128,128]{1,0:T(8,128)S(1)} %copy-done.5, s32[1,128]{1,0:T(1,128)S(1)} %bitcast.1, s32[128,128]{1,0:T(8,128)S(1)} %copy-done.6, ...), custom_call_target="tpu_custom_call" | custom-call | tf_op jit(solution)/shard_map/pallas_call | solution.py:391
  109.9 0.7 copy.13
  110.6 0.7 copy.14
Async XLA Ops:
  0.6 0.7 copy-start.8
  1.3 1.0 copy-start
  2.3 1.0 copy-start.1
  3.3 0.9 copy-start.2
  4.2 0.9 copy-start.3
  5.2 0.9 copy-start.4
  6.1 0.8 copy-start.5
  7.0 0.8 copy-start.6
  7.8 0.7 copy-start.7

commit v2 on v1

v2 whole, which is shorter than its diff:
```python
import functools

import jax
import jax.numpy as jnp
import numpy as np
from jax import lax
from jax.experimental import pallas as pl
from jax.experimental.pallas import tpu as pltpu
from jax.sharding import PartitionSpec as P

ITERS = 3
TYPES = 4
SHIFTS = 4
OMEGA = 0.05
MESH = pl.DeviceIdType.MESH
F32 = jnp.float32
BF16 = jnp.bfloat16


def split(x):
    high = x.astype(BF16)
    low = (x - high.astype(F32)).astype(BF16)
    return high, low


def tables(harmonics):
    samples = 2 * harmonics
    row = np.arange(2 * harmonics)
    wave = (row // 4) * 2 + row % 2
    part = (row // 2) % 2
    moment = np.arange(samples)
    phase = (moment[:, None] * wave[None, :] % samples) * (2.0 * np.pi / samples)
    inverse = np.where(part[None, :] == 0, np.cos(phase), -np.sin(phase))
    weight = np.where(wave == 0, 1.0, 2.0) / samples
    forward = inverse.T * weight[:, None]

    def stacked(matrix):
        matrix = matrix.astype(np.float32)
        high = matrix.astype(jnp.bfloat16)
        low = (matrix - high.astype(np.float32)).astype(jnp.bfloat16)
        return np.concatenate([high, low], axis=0)

    return stacked(inverse), stacked(forward)


def kernel(
    state_hbm, source_hbm, cap_hbm, shift_hbm, kinds_hbm, table, precond_hbm, inv_hbm, fwd_hbm,
    out_update, out_resid,
    state, source, cap, shift, kinds, precond, inv, fwd,
    weights, slopes, basis, images, directions,
    t_send, t_recv, l_send, l_recv, halo_send, halo_recv, ar_send, ar_recv, ax_send, ax_recv,
    in_sem, t_ssem, t_rsem, l_ssem, l_rsem, h_ssem, h_rsem, a_ssem, a_rsem, x_ssem, x_rsem,
):
    harm = lax.axis_index("harm")
    node = lax.axis_index("node")
    y, z, core = harm // 16, lax.rem(harm // 2, 8), lax.rem(harm, 2)
    inputs = [
        (state_hbm, state), (inv_hbm, inv), (kinds_hbm, kinds), (fwd_hbm, fwd),
        (precond_hbm, precond), (shift_hbm, shift), (cap_hbm, cap), (source_hbm, source),
    ]
    loads = [pltpu.make_async_copy(a, b, in_sem.at[i]) for i, (a, b) in enumerate(inputs)]
    for load in loads:
        load.start()

    y_parts = [lax.rem(y + dy, 4) * 16 for dy in range(4)]
    c_parts = [lax.rem(core + dc, 2) for dc in range(2)]
    near = [(dy, dc) for dy in (2, 1, 3, 0) for dc in (1, 0)]

    def each_peer(act):
        @pl.loop(0, 7)
        def _(i):
            dz = jnp.where(lax.rem(i, 2) == 0, 4 + i // 2, 4 - (i + 1) // 2)
            z_part = lax.rem(z + dz, 8) * 2
            for dy, dc in near:
                act(y_parts[dy] + z_part + c_parts[dc])

        for dy, dc in near[:-1]:
            act(y_parts[dy] + z * 2 + c_parts[dc])

    barrier = pltpu.get_barrier_semaphore()

    def greet(other):
        pl.semaphore_signal(barrier, inc=1, device_id=(other, node), device_id_type=MESH)

    each_peer(greet)
    for d in (1, 2, 3):
        pl.semaphore_signal(
            barrier, inc=1, device_id=(harm, lax.rem(node + d, 4)), device_id_type=MESH
        )

    def unit(index):
        return pl.ds(pl.multiple_of(index * 4, 4), 4)

    def exchange(send, recv, ssem, rsem, stage, half):
        def push(other):
            pltpu.make_async_remote_copy(
                src_ref=send.at[stage, half, unit(other)],
                dst_ref=recv.at[stage, half, unit(harm)],
                send_sem=ssem.at[stage, half],
                recv_sem=rsem.at[stage, half],
                device_id=(other, node),
                device_id_type=MESH,
            ).start()

        each_peer(push)
        recv[stage, half, unit(harm), :] = send[stage, half, unit(harm), :]

    def arrived(send, recv, ssem, rsem, stage, half):
        return pltpu.make_async_remote_copy(
            src_ref=send.at[stage, half, pl.ds(0, 252)],
            dst_ref=recv.at[stage, half, pl.ds(0, 252)],
            send_sem=ssem.at[stage, half],
            recv_sem=rsem.at[stage, half],
            device_id=(lax.rem(harm + 1, 64), node),
            device_id_type=MESH,
        )

    t_all = (t_send, t_recv, t_ssem, t_rsem)
    l_all = (l_send, l_recv, l_ssem, l_rsem)

    def halo_copy(stage, side):
        step = 1 if side == 0 else 3
        return pltpu.make_async_remote_copy(
            src_ref=halo_send.at[stage, side],
            dst_ref=halo_recv.at[stage, side],
            send_sem=h_ssem.at[stage, side],
            recv_sem=h_rsem.at[stage, side],
            device_id=(harm, lax.rem(node + step, 4)),
            device_id_type=MESH,
        )

    pairs = [(p, kk) for p in range(2) for kk in range(2)]
    halves = [slice(0, 64), slice(64, 128)]

    def to_time(field, stage, half):
        for p, kk in pairs:
            t_send[stage, half, pl.ds(p * 2 + kk, 64, stride=4), :] = field[p, kk, halves[half], :]

    def send_halo(field, stage):
        last = [field[p, kk, 127:128, :] for p, kk in pairs]
        first = [field[p, kk, 0:1, :] for p, kk in pairs]
        halo_send[stage, 0] = jnp.concatenate(last + last, axis=0)
        halo_send[stage, 1] = jnp.concatenate(first + first, axis=0)
        for side in range(2):
            halo_copy(stage, side).start()

    def product(matrix, x):
        high, low = split(x)
        all_parts = jnp.dot(
            matrix[...], jnp.concatenate([high, low], axis=1), preferred_element_type=F32
        )
        return (all_parts[0:256, 0:128] + all_parts[0:256, 128:256]) + all_parts[256:512, 0:128]

    def time_of(stage, half):
        return product(inv, t_recv[stage, half])

    def to_spec(signal, stage, half):
        l_send[stage, half] = product(fwd, signal)
        exchange(*l_all, stage, half)

    def spec_part(stage, half, p, kk):
        return l_recv[stage, half, pl.ds(p * 2 + kk, 64, stride=4), :]

    loads[0].wait()
    to_time(state, 0, 0)
    pl.semaphore_wait(barrier, 66)
    exchange(*t_all, 0, 0)
    to_time(state, 0, 1)
    exchange(*t_all, 0, 1)
    send_halo(state, 0)

    for load in loads[1:]:
        load.wait()
    for kk in range(2):
        both = jnp.concatenate([precond[0, kk].T, precond[1, kk].T], axis=1)
        high, low = split(both)
        weights[kk, 0:128, :] = high
        weights[kk, 128:256, :] = low
    params = []
    for half in range(2):
        kind = kinds[pl.ds(harm + half * 64, 1), :]
        params.append(
            [
                sum(jnp.where(kind == member, table[what, member], 0.0) for member in range(TYPES))
                for what in range(3)
            ]
        )
    shifts = jnp.broadcast_to(shift[...].astype(F32), (128, 128)).T
    row = lax.broadcasted_iota(jnp.int32, (128, 128), 0)
    waves = [(2 * harm + kk).astype(F32) * OMEGA for kk in range(2)]
    not_first = jnp.where(node == 0, 0.0, 1.0)
    not_last = jnp.where(node == 3, 0.0, 1.0)

    def stencil(field, stage, p, kk):
        f = field[p, kk]
        index = p * 2 + kk
        halo_a = halo_recv[stage, 0, index : index + 1, :] * not_first
        halo_b = halo_recv[stage, 1, index : index + 1, :] * not_last
        above = jnp.where(row == 0, halo_a, pltpu.roll(f, 1, axis=0))
        below = jnp.where(row == 127, halo_b, pltpu.roll(f, 127, axis=0))
        skewed = above
        for amount in range(1, SHIFTS):
            skewed = jnp.where(
                shifts == float(amount), pltpu.roll(above, 128 - amount, axis=1), skewed
            )
        sides = pltpu.roll(f, 1, axis=1) + pltpu.roll(f, 127, axis=1)
        result = 4.0 * f - sides - skewed - below
        turned = waves[kk] * cap[...] * field[1 - p, kk]
        return result - turned if p == 0 else result + turned

    def halo_wait(stage):
        for side in range(2):
            halo_copy(stage, side).wait_recv()

    zero = jnp.zeros((128, 128), BF16)

    def precondition(field, target, half):
        part = halves[half]
        for kk in range(2):
            high, low = split(
                jnp.concatenate([field[0, kk, part, :], field[1, kk, part, :]], axis=0)
            )
            left = jnp.concatenate(
                [
                    jnp.concatenate([high, high], axis=1),
                    jnp.concatenate([low, zero], axis=1),
                ],
                axis=0,
            )
            out = jnp.dot(left, weights[kk], preferred_element_type=F32)
            out = out[0:128] + out[128:256]
            target[0, kk, part, :] = out[0:64, 0:128] - out[64:128, 128:256]
            target[1, kk, part, :] = out[0:64, 128:256] + out[64:128, 0:128]

    lane = lax.broadcasted_iota(jnp.int32, (1, 128), 1)

    def inner(a, b):
        total = sum(a[p, kk] * b[p, kk] for p, kk in pairs)
        return jnp.sum(jnp.sum(total, axis=0, keepdims=True), axis=1, keepdims=True)

    def reduce_start(stage, values):
        packed = sum(jnp.where(lane == q, value, 0.0) for q, value in enumerate(values))
        ar_send[stage] = packed

        def push(other):
            pltpu.make_async_remote_copy(
                src_ref=ar_send.at[stage],
                dst_ref=ar_recv.at[stage, harm],
                send_sem=a_ssem.at[stage],
                recv_sem=a_rsem.at[stage],
                device_id=(other, node),
                device_id_type=MESH,
            ).start()

        each_peer(push)
        ar_recv[stage, harm] = packed

    def reduce_all(stage):
        return pltpu.make_async_remote_copy(
            src_ref=ar_recv.at[stage, pl.ds(0, 63)],
            dst_ref=ar_recv.at[stage, pl.ds(0, 63)],
            send_sem=a_ssem.at[stage],
            recv_sem=a_rsem.at[stage],
            device_id=(lax.rem(harm + 1, 64), node),
            device_id_type=MESH,
        )

    def ax_copy(stage, d):
        return pltpu.make_async_remote_copy(
            src_ref=ax_send.at[stage],
            dst_ref=ax_recv.at[stage, node],
            send_sem=x_ssem.at[stage, d],
            recv_sem=x_rsem.at[stage, d],
            device_id=(harm, lax.rem(node + d + 1, 4)),
            device_id_type=MESH,
        )

    def reduce_middle(stage):
        reduce_all(stage).wait_recv()
        total = jnp.sum(ar_recv[stage], axis=0)
        ax_send[stage] = total
        for d in range(3):
            ax_copy(stage, d).start()
        ax_recv[stage, node] = total

    def reduce_finish(stage):
        for d in range(3):
            ax_copy(stage, d).wait_recv()
        total = jnp.sum(ax_recv[stage], axis=0)
        return lambda q: total[:, q : q + 1]

    def evaluate(half):
        linear, amplitude, slope = params[half]
        arrived(*t_all, 0, half).wait_recv()
        voltage = time_of(0, half)
        bent = jnp.tanh(slope * voltage)
        slopes[half] = linear + amplitude * slope * (1.0 - bent * bent)
        to_spec(linear * voltage + amplitude * bent, 0, half)

    p0 = basis.at[0]
    evaluate(0)
    halo_wait(0)
    for p, kk in pairs:
        basis[0, p, kk] = source[p, kk] - stencil(state, 0, p, kk)
    evaluate(1)
    z0, z1, z2 = [directions.at[j] for j in range(3)]
    i0, i1, i2 = [images.at[j] for j in range(3)]
    for half, part in enumerate(halves):
        arrived(*l_all, 0, half).wait_recv()
        for p, kk in pairs:
            basis[0, p, kk, part, :] = basis[0, p, kk, part, :] - spec_part(0, half, p, kk)
        precondition(p0, z0, half)
        to_time(z0, 1, half)
        exchange(*t_all, 1, half)
    send_halo(z0, 1)
    for p, kk in pairs:
        out_resid[p, kk] = -basis[0, p, kk]

    def apply_time(stage, half):
        arrived(*t_all, stage, half).wait_recv()
        to_spec(slopes[half] * time_of(stage, half), stage, half)

    def middle(stage):
        apply_time(stage, 0)
        halo_wait(stage)
        for p, kk in pairs:
            images[stage - 1, p, kk] = stencil(directions.at[stage - 1], stage, p, kk)
        apply_time(stage, 1)

    def finish_image(stage, half):
        part = halves[half]
        arrived(*l_all, stage, half).wait_recv()
        for p, kk in pairs:
            images[stage - 1, p, kk, part, :] = (
                images[stage - 1, p, kk, part, :] + spec_part(stage, half, p, kk)
            )

    def finish_and_send(stage):
        for half in range(2):
            finish_image(stage, half)
            precondition(images.at[stage - 1], directions.at[stage], half)
            to_time(directions.at[stage], stage + 1, half)
            exchange(*t_all, stage + 1, half)
        send_halo(directions.at[stage], stage + 1)

    middle(1)
    finish_and_send(1)

    reduce_start(0, [inner(p0, p0), inner(p0, i0), inner(i0, i0)])
    middle(2)
    reduce_middle(0)
    first = reduce_finish(0)
    h = first(1) / first(0)
    for p, kk in pairs:
        images[1, p, kk] = i1[p, kk] - h * i0[p, kk]
    finish_and_send(2)
    for p, kk in pairs:
        basis[1, p, kk] = i0[p, kk] - h * p0[p, kk]
        directions[1, p, kk] = z1[p, kk] - h * z0[p, kk]

    p1 = basis.at[1]
    reduce_start(
        1, [inner(p0, i1), inner(p1, i1), inner(p1, p1), inner(i0, i1), inner(i1, i1)]
    )
    middle(3)
    reduce_middle(1)
    second = reduce_finish(1)
    h0, h1 = second(0) / first(0), second(1) / second(2)
    for p, kk in pairs:
        images[2, p, kk] = i2[p, kk] - h0 * i0[p, kk] - h1 * i1[p, kk]
    finish_image(3, 0)
    finish_image(3, 1)
    reduce_start(2, [inner(p0, i2), inner(i0, i2), inner(i1, i2), inner(i2, i2)])
    for p, kk in pairs:
        directions[2, p, kk] = z2[p, kk] - h0 * z0[p, kk] - h1 * z1[p, kk]
    reduce_middle(2)
    third = reduce_finish(2)

    g00, g01, g02 = first(2), second(3), third(1)
    g11, g12, g22 = second(4), third(2), third(3)
    b0, b1, b2 = first(1), second(0), third(0)
    l10, l20 = g01 / g00, g02 / g00
    d1 = g11 - l10 * g01
    e12 = g12 - l10 * g02
    c1 = b1 - l10 * b0
    l21 = e12 / d1
    d2 = g22 - l20 * g02 - l21 * e12
    c2 = b2 - l20 * b0 - l21 * c1
    y2 = c2 / d2
    y1 = (c1 - e12 * y2) / d1
    y0 = (b0 - g01 * y1 - g02 * y2) / g00
    for p, kk in pairs:
        out_update[p, kk] = y0 * z0[p, kk] + y1 * z1[p, kk] + y2 * z2[p, kk]

    for stage in range(4):
        for half in range(2):
            arrived(*t_all, stage, half).wait_send()
            arrived(*l_all, stage, half).wait_send()
        for side in range(2):
            halo_copy(stage, side).wait_send()
    for stage in range(3):
        reduce_all(stage).wait_send()
        for d in range(3):
            ax_copy(stage, d).wait_send()


def body(state, source, capacity, row_shift, device_type, device_table, precond):
    inverse, forward = tables(state.shape[1] * lax.axis_size("harm"))
    block = (2, 2, 128, 128)
    vmem = pltpu.VMEM
    dma = pltpu.SemaphoreType.DMA
    hbm = pl.BlockSpec(memory_space=pltpu.HBM)
    update, resid = pl.pallas_call(
        kernel,
        out_shape=[jax.ShapeDtypeStruct(block, F32)] * 2,
        in_specs=[hbm] * 5 + [pl.BlockSpec(memory_space=pltpu.SMEM)] + [hbm] * 3,
        out_specs=[pl.BlockSpec(memory_space=vmem)] * 2,
        scratch_shapes=[
            vmem(block, F32), vmem(block, F32), vmem((128, 128), F32), vmem((1, 128), jnp.int32),
            vmem((128, 128), jnp.int32), vmem(block, F32), vmem((512, 256), BF16),
            vmem((512, 256), BF16),
            vmem((2, 256, 256), BF16), vmem((2, 256, 128), F32), vmem((2,) + block, F32),
            vmem((3,) + block, F32), vmem((3,) + block, F32),
            vmem((4, 2, 256, 128), F32), vmem((4, 2, 256, 128), F32),
            vmem((4, 2, 256, 128), F32), vmem((4, 2, 256, 128), F32),
            vmem((4, 2, 8, 128), F32), vmem((4, 2, 8, 128), F32),
            vmem((3, 1, 128), F32), vmem((3, 64, 1, 128), F32),
            vmem((3, 1, 128), F32), vmem((3, 4, 1, 128), F32),
            dma((8,)), dma((4, 2)), dma((4, 2)), dma((4, 2)), dma((4, 2)),
            dma((4, 2)), dma((4, 2)), dma((3,)), dma((3,)), dma((3, 3)), dma((3, 3)),
        ],
        compiler_params=pltpu.CompilerParams(
            collective_id=0, has_side_effects=True, vmem_limit_bytes=67_000_000
        ),
    )(
        state, source, capacity, row_shift.reshape(1, -1), device_type, device_table, precond,
        jnp.asarray(inverse), jnp.asarray(forward),
    )
    return update, resid


def solution(mesh):
    harm, node = mesh.axis_names
    return jax.shard_map(
        body,
        mesh=mesh,
        in_specs=(
            P(None, harm, node, None),
            P(None, harm, node, None),
            P(node, None),
            P(node),
            P(node, None),
            P(),
            P(None, harm, None, None),
        ),
        out_specs=(P(None, harm, node, None), P(None, harm, node, None)),
        check_vma=False,
    )
```

time: 112 us -> 87.8 us (0.78)
  Pallas kernels: 101 us -> 84.6 us
  local copies, waits for them, and re-layouts: 9.25 us -> 2.42 us
    pallas_call x1, Pallas kernels: 101 us -> 84.6 us  [body(): pl.pallas_call(kernel, out_shape=[jax.ShapeDtypeStruct(block, F32)] * 2,...]
    unnamed x20 -> x4, local copies, waits for them, and re-layouts: 9.25 us -> 2.42 us
where the time goes in v2:
time: 87.8 us; the launch traced here: 87.7 us
  Pallas kernels  84.6 us (96%)
  local copies, waits for them, and re-layouts  2.42 us (3%)
    pallas_call x1, Pallas kernels, body(): pl.pallas_call(kernel, out_shape=[jax.ShapeDtypeStruct(block, F32)] * 2,...  84.6 us
    unnamed x4, local copies, waits for them, and re-layouts  2.42 us

profile of v2, /device:TPU:1, one launch (start us, length us, event | category | flops | bytes accessed | tf_op | source)
XLA Modules:
  0.0 87.7 jit_solution(14793532561930876260)
XLA Ops:
  0.6 84.6 %shard_map.104 = (f32[2,2,128,128]{3,2,1,0:T(8,128)}, f32[2,2,128,128]{3,2,1,0:T(8,128)}) custom-call(f32[2,2,128,128]{3,2,1,0:T(8,128)} %state_hbm.1, f32[2,2,128,128]{3,2,1,0:T(8,128)} %source_hbm.1, f32[128,128]{1,0:T(8,128)} %cap_hbm.1, s32[1,128]{1,0:T(1,128)} %bitcast.1, s32[128,128]{1,0:T(8,128)} %kinds_hbm.1, f32[3,4]{1,0:T(4,128)} %table.1, ...), custom_call_target="tpu_custom_call" | custom-call | tf_op jit(solution)/shard_map/pallas_call | solution.py:413
  85.3 0.0 copy-start
  85.3 1.7 %copy.13 = f32[2,2,128,128]{3,2,1,0:T(8,128)} copy(f32[2,2,128,128]{3,2,1,0:T(8,128)} %get-tuple-element.4) | data formatting | bytes 524288
  87.0 0.0 copy-done
  87.0 0.7 copy.14
Async XLA Ops:
  85.3 1.7 %copy-start = (f32[2,2,128,128]{3,2,1,0:T(8,128)S(1)}, f32[2,2,128,128]{3,2,1,0:T(8,128)}, u32[]{:S(2)}) copy-start(f32[2,2,128,128]{3,2,1,0:T(8,128)} %get-tuple-element.5) | copy-start | bytes 786436

commit v3 on v2

v3 whole, which is shorter than its diff:
```python
import functools

import jax
import jax.numpy as jnp
import numpy as np
from jax import lax
from jax.experimental import pallas as pl
from jax.experimental.pallas import tpu as pltpu
from jax.sharding import PartitionSpec as P

ITERS = 3
TYPES = 4
SHIFTS = 4
FOLD = 1
OMEGA = 0.05
MESH = pl.DeviceIdType.MESH
F32 = jnp.float32
BF16 = jnp.bfloat16


def split(x):
    high = x.astype(BF16)
    low = (x - high.astype(F32)).astype(BF16)
    return high, low


def tables(harmonics):
    samples = 2 * harmonics
    row = np.arange(2 * harmonics)
    slot, q = row // 4, row % 4
    z_high, rest = slot % (8 // FOLD), slot // (8 // FOLD)
    z_low, y, core = rest // 8, rest // 2 % 4, rest % 2
    harm = y * 16 + (z_high * FOLD + z_low) * 2 + core
    wave, part = 2 * harm + q % 2, q // 2
    moment = np.arange(samples)
    phase = (moment[:, None] * wave[None, :] % samples) * (2.0 * np.pi / samples)
    inverse = np.where(part[None, :] == 0, np.cos(phase), -np.sin(phase))
    weight = np.where(wave == 0, 1.0, 2.0) / samples
    forward = inverse.T * weight[:, None]

    def stacked(matrix):
        matrix = matrix.astype(np.float32)
        high = matrix.astype(jnp.bfloat16)
        low = (matrix - high.astype(np.float32)).astype(jnp.bfloat16)
        return np.concatenate([high, low], axis=0)

    return stacked(inverse), stacked(forward)


def kernel(
    state_hbm, source_hbm, cap_hbm, shift_hbm, kinds_hbm, table, precond_hbm, inv_hbm, fwd_hbm,
    update_hbm, resid_hbm,
    state, source, cap, shift, kinds, precond, inv, fwd,
    gathered, weights, slopes, shifts, start, start_rows, first_z, direct, images,
    direct_back, out_update, out_resid,
    ta_send, ta_recv, la_send, la_recv, zf_recv, lg_send, lg_recv, tg_send, tg_recv,
    halo_send, halo_recv, ring_send, ring_recv, ar_send, ar_recv, ax_send, ax_recv,
    in_sem, out_sem, ta_ssem, ta_rsem, la_ssem, la_rsem, zf_ssem, zf_rsem, lg_ssem, lg_rsem, tg_ssem,
    tg_rsem, h_ssem, h_rsem, r_ssem, r_rsem, gz_ssem, gz_rsem, gx_ssem, gx_rsem, b_ssem, b_rsem,
    a_ssem, a_rsem, x_ssem, x_rsem,
):
    harm = lax.axis_index("harm")
    node = lax.axis_index("node")
    y, z, core = harm // 16, lax.rem(harm // 2, 8), lax.rem(harm, 2)
    chunks = 8 // FOLD
    group = 8 * FOLD
    zh, zl = z // FOLD, lax.rem(z, FOLD)
    mine = zl * 8 + y * 2 + core
    slot = mine * chunks + zh
    inputs = [
        (state_hbm, state), (precond_hbm, precond), (inv_hbm, inv), (kinds_hbm, kinds),
        (fwd_hbm, fwd), (shift_hbm, shift), (cap_hbm, cap), (source_hbm, source),
    ]
    loads = [pltpu.make_async_copy(a, b, in_sem.at[i]) for i, (a, b) in enumerate(inputs)]
    for load in loads:
        load.start()

    ys = [lax.rem(y + dy, 4) for dy in range(4)]
    cs = [lax.rem(core + dc, 2) for dc in range(2)]
    near = [(dy, dc) for dy in (2, 1, 3, 0) for dc in (1, 0)]

    def each_peer(act):
        @pl.loop(0, 7)
        def _(i):
            dz = jnp.where(lax.rem(i, 2) == 0, 4 + i // 2, 4 - (i + 1) // 2)
            other = lax.rem(z + dz, 8)
            base = other // FOLD + lax.rem(other, FOLD) * 8 * chunks
            for dy, dc in near:
                place = ys[dy] * 2 + cs[dc]
                act(ys[dy] * 16 + other * 2 + cs[dc], base + place * chunks)

        for dy, dc in near[:-1]:
            act(
                ys[dy] * 16 + z * 2 + cs[dc],
                zh + (zl * 8 + ys[dy] * 2 + cs[dc]) * chunks,
            )

    def each_mate(act):
        for dl in reversed(range(FOLD)):
            for dy, dc in near:
                if dl or dy or dc:
                    low = lax.rem(zl + dl, FOLD)
                    act(
                        ys[dy] * 16 + (zh * FOLD + low) * 2 + cs[dc],
                        low * 8 + ys[dy] * 2 + cs[dc],
                    )

    def along(d):
        high = lax.rem(zh + d, chunks)
        return y * 16 + (high * FOLD + zl) * 2 + core, high

    next_harm, prev_harm = along(1)[0], along(chunks - 1)[0]
    next_node = lax.rem(node + jnp.where(zh == chunks - 1, 1, 0), 4)
    prev_node = lax.rem(node + jnp.where(zh == 0, 3, 0), 4)
    ring = [(next_harm, next_node), (prev_harm, prev_node)]

    barrier = pltpu.get_barrier_semaphore()

    def greet(other, _):
        pl.semaphore_signal(barrier, inc=1, device_id=(other, node), device_id_type=MESH)

    each_peer(greet)
    for d in (1, 2, 3):
        pl.semaphore_signal(
            barrier, inc=1, device_id=(harm, lax.rem(node + d, 4)), device_id_type=MESH
        )
    for place in ring:
        pl.semaphore_signal(barrier, inc=1, device_id=place, device_id_type=MESH)

    def copy(src, dst, ssem, rsem, place):
        return pltpu.make_async_remote_copy(
            src_ref=src, dst_ref=dst, send_sem=ssem, recv_sem=rsem,
            device_id=place, device_id_type=MESH,
        )

    def unit(index):
        return pl.ds(pl.multiple_of(index * 4, 4), 4)

    def exchange(bufs, at):
        send, recv, ssem, rsem = bufs

        def push(other, other_slot):
            copy(
                send.at[*at, unit(other_slot)], recv.at[*at, unit(slot)],
                ssem.at[*at], rsem.at[*at], (other, node),
            ).start()

        each_peer(push)
        recv[*at, unit(slot), :] = send[*at, unit(slot), :]

    def exchanged(bufs, at):
        send, recv, ssem, rsem = bufs
        rows = pl.ds(0, 252)
        return copy(
            send.at[*at, rows], recv.at[*at, rows], ssem.at[*at], rsem.at[*at], (prev_harm, node)
        )

    wide = 4 * chunks

    def share(bufs, at):
        send, recv, ssem, rsem = bufs
        own = pl.ds(pl.multiple_of(mine * wide, wide), wide)

        def push(other, place):
            copy(
                send.at[*at, pl.ds(pl.multiple_of(place * wide, wide), wide)], recv.at[*at, own],
                ssem.at[*at], rsem.at[*at], (other, node),
            ).start()

        each_mate(push)
        recv[*at, own, :] = send[*at, own, :]

    def shared(bufs, at):
        send, recv, ssem, rsem = bufs
        rows = pl.ds(0, 256 - wide)
        return copy(
            send.at[*at, rows], recv.at[*at, rows],
            ssem.at[*at], rsem.at[*at], (prev_harm, node),
        )

    def spread(c, q):
        return pl.ds(c * 4 + q, group, stride=wide)

    ta = (ta_send, ta_recv, ta_ssem, ta_rsem)
    la = (la_send, la_recv, la_ssem, la_rsem)
    zf = (ta_recv.at[1], zf_recv, zf_ssem, zf_rsem)
    lg = (lg_send, lg_recv, lg_ssem, lg_rsem)
    tg = (tg_send, tg_recv, tg_ssem, tg_rsem)

    def halo_copy(side):
        step = 1 if side == 0 else 3
        return copy(
            halo_send.at[side], halo_recv.at[side], h_ssem.at[side], h_rsem.at[side],
            (harm, lax.rem(node + step, 4)),
        )

    def ring_copy(stage, side):
        return copy(
            ring_send.at[stage, side], ring_recv.at[stage, side],
            r_ssem.at[stage, side], r_rsem.at[stage, side], ring[side],
        )

    pairs = [(p, kk) for p in range(2) for kk in range(2)]
    deep = 2 * group

    def strip(chunk, half):
        return slice(chunk * deep + half * group, chunk * deep + (half + 1) * group)

    def to_time(field, stage, half):
        for p, kk in pairs:
            for c in range(chunks):
                ta_send[stage, half, spread(c, p * 2 + kk), :] = field[p, kk, strip(c, half), :]

    def product(matrix, x):
        high, low = split(x)
        all_parts = jnp.dot(
            matrix[...], jnp.concatenate([high, low], axis=1), preferred_element_type=F32
        )
        return (all_parts[0:256, 0:128] + all_parts[0:256, 128:256]) + all_parts[256:512, 0:128]

    loads[0].wait()
    to_time(state, 0, 0)
    loads[1].wait()
    for kk in range(2):
        gathered[zh, kk, :, 0:128] = precond[0, kk].T
        gathered[zh, kk, :, 128:256] = precond[1, kk].T

    def build(high_place):
        for kk in range(2):
            high, low = split(gathered[high_place, kk])
            weights[high_place, kk, 0:128, :] = high
            weights[high_place, kk, 128:256, :] = low

    build(zh)
    for load in loads[2:]:
        load.wait()
    params = []
    for half in range(2):
        kind = kinds[pl.ds(zh * deep + half * group + mine, 1), :]
        params.append(
            [
                sum(jnp.where(kind == member, table[what, member], 0.0) for member in range(TYPES))
                for what in range(3)
            ]
        )
    shifts[...] = jnp.broadcast_to(shift[...].astype(F32), (128, 128)).T

    pl.semaphore_wait(barrier, 68)
    exchange(ta, (0, 0))
    to_time(state, 0, 1)
    exchange(ta, (0, 1))
    last = [state[p, kk, 127:128, :] for p, kk in pairs]
    first = [state[p, kk, 0:1, :] for p, kk in pairs]
    halo_send[0] = jnp.concatenate(last + last, axis=0)
    halo_send[1] = jnp.concatenate(first + first, axis=0)
    for side in range(2):
        halo_copy(side).start()

    quarter = pl.ds(pl.multiple_of(node * 32, 32), 32)

    def along_z(way, step):
        high = along(step - 1 if way else chunks - (step - 1) if step > 1 else 0)[1]
        place = gathered.at[high, :, quarter]
        index = 4 * way + step - 1
        target = along(chunks - 1 if way else 1)[0]
        return copy(place, place, gz_ssem.at[index], gz_rsem.at[index], (target, node))

    def along_x(way, step, dx):
        high = along(step if way else chunks - step)[1]
        place = gathered.at[high, :, quarter]
        index = 4 * way + step - 1
        return copy(
            place, place, gx_ssem.at[index, dx - 1], gx_rsem.at[index, dx - 1],
            (harm, lax.rem(node + dx, 4)),
        )

    moves = [(way, step) for step in (1, 2, 3, 4) for way in (0, 1) if way == 0 or step < 4]

    def pass_on(step):
        for way, at in moves:
            if at == step:
                along_z(way, at).wait_recv()
        for way, at in moves:
            if at == step + 1:
                along_z(way, at).start()
        for dx in (2, 1, 3):
            for way, at in moves:
                if at == step:
                    along_x(way, at, dx).start()

    def receive(step):
        for way, at in moves:
            if at == step:
                for dx in (1, 2, 3):
                    along_x(way, at, dx).wait_recv()
                build(along(at if way else chunks - at)[1])

    for way, at in moves:
        if at == 1:
            along_z(way, at).start()

    def stencil(f, turned, halo_a, halo_b, shift_rows):
        rows = f.shape[0]
        row = lax.broadcasted_iota(jnp.int32, (rows, 128), 0)
        above = jnp.where(row == 0, halo_a, pltpu.roll(f, 1, axis=0))
        below = jnp.where(row == rows - 1, halo_b, pltpu.roll(f, rows - 1, axis=0))
        skewed = above
        for amount in range(1, SHIFTS):
            skewed = jnp.where(
                shift_rows == float(amount), pltpu.roll(above, 128 - amount, axis=1), skewed
            )
        sides = pltpu.roll(f, 1, axis=1) + pltpu.roll(f, 127, axis=1)
        return 4.0 * f - sides - skewed - below + turned

    zero = jnp.zeros((128, 128), BF16)

    def complex_product(u0, u1, weight):
        rows = u0.shape[0]
        high, low = split(jnp.concatenate([u0, u1], axis=0))
        left = jnp.concatenate(
            [
                jnp.concatenate([high, high], axis=1),
                jnp.concatenate([low, zero[0 : 2 * rows]], axis=1),
            ],
            axis=0,
        )
        out = jnp.dot(left, weight, preferred_element_type=F32)
        out = out[0 : 2 * rows] + out[2 * rows : 4 * rows]
        real = out[0:rows, 0:128] - out[rows : 2 * rows, 128:256]
        imag = out[0:rows, 128:256] + out[rows : 2 * rows, 0:128]
        return real, imag

    def evaluate(half):
        linear, amplitude, slope = params[half]
        exchanged(ta, (0, half)).wait_recv()
        voltage = product(inv, ta_recv[0, half])
        bent = jnp.tanh(slope * voltage)
        slopes[half] = linear + amplitude * slope * (1.0 - bent * bent)
        la_send[half] = product(fwd, linear * voltage + amplitude * bent)
        exchange(la, (half,))

    evaluate(0)
    for side in range(2):
        halo_copy(side).wait_recv()
    not_first = jnp.where(node == 0, 0.0, 1.0)
    not_last = jnp.where(node == 3, 0.0, 1.0)
    for p, kk in pairs:
        index = p * 2 + kk
        wave = (2 * harm + kk).astype(F32) * (-OMEGA if p == 0 else OMEGA)
        start[index] = source[p, kk] - stencil(
            state[p, kk],
            wave * cap[...] * state[1 - p, kk],
            halo_recv[0, index : index + 1, :] * not_first,
            halo_recv[1, index : index + 1, :] * not_last,
            shifts[...],
        )
    evaluate(1)
    pass_on(1)
    for half in range(2):
        exchanged(la, (half,)).wait_recv()
        for q in range(4):
            for c in range(chunks):
                part = strip(c, half)
                start[q, part, :] = start[q, part, :] - la_recv[half, spread(c, q), :]
        for kk in range(2):
            u0, u1 = [
                jnp.concatenate([start[q, strip(c, half), :] for c in range(chunks)], axis=0)
                for q in (kk, 2 + kk)
            ]
            real, imag = complex_product(u0, u1, weights[zh, kk])
            for q, value in ((kk, real), (2 + kk, imag)):
                for c in range(chunks):
                    piece = value[c * group : (c + 1) * group]
                    ta_send[1, half, spread(c, q), :] = piece
                    first_z[q, strip(c, half), :] = piece
        exchange(ta, (1, half))
        if half == 0:
            pass_on(2)
    receive(1)
    for p, kk in pairs:
        out_resid[p, kk] = -start[p * 2 + kk]
    resid_out = pltpu.make_async_copy(out_resid, resid_hbm, out_sem.at[4])
    resid_out.start()
    def to_spec(signal, stage, half):
        lg_send[stage, half] = product(fwd, signal)
        share(lg, (stage, half))

    for half in range(2):
        exchanged(ta, (1, half)).wait_recv()
        share(zf, (half,))
        to_spec(slopes[half] * product(inv, ta_recv[1, half]), 0, half)
        pass_on(3 + half)
    receive(2)

    def start_copy(d):
        other, high = along(d)
        return copy(
            start.at[:, pl.ds(pl.multiple_of(high * deep, deep), deep)], start_rows.at[zh],
            b_ssem.at[0, d - 1], b_rsem.at[0, d - 1], (other, node),
        )

    def back_copy(which, d):
        other, high = along(d)
        size = 4 * deep
        return copy(
            direct.at[which, pl.ds(pl.multiple_of(high * size, size), size)],
            direct_back.at[which - 1, pl.ds(pl.multiple_of(zh * size, size), size)],
            b_ssem.at[which, d - 1], b_rsem.at[which, d - 1], (other, node),
        )

    start_rows[zh] = start[:, pl.ds(pl.multiple_of(zh * deep, deep), deep), :]

    fields = [(c, q) for c in range(chunks) for q in range(4)]

    def at_rows(c, q, half=None):
        first_row = (c * 4 + q) * deep
        if half is None:
            return pl.ds(first_row, deep)
        return pl.ds(first_row + half * group, group)

    def send_ring(which):
        ring_send[which, 0] = direct[which, pl.ds(deep - 1, 4 * chunks, stride=deep), :]
        ring_send[which, 1] = direct[which, pl.ds(0, 4 * chunks, stride=deep), :]
        for side in range(2):
            ring_copy(which, side).start()

    chunk = pl.ds(pl.multiple_of(zh * deep, deep), deep)
    has_above = jnp.where((node == 0) & (zh == 0), 0.0, 1.0)
    has_below = jnp.where((node == 3) & (zh == chunks - 1), 0.0, 1.0)

    def local_image(which):
        for side in range(2):
            ring_copy(which, side).wait_recv()
        cap_rows, shift_rows = cap[chunk, :], shifts[chunk, :]
        for c, q in fields:
            p, kk = q // 2, q % 2
            place = y * 16 + (c * FOLD + zl) * 2 + core
            wave = (2 * place + kk).astype(F32) * (-OMEGA if p == 0 else OMEGA)
            index = c * 4 + q
            images[which, at_rows(c, q), :] = stencil(
                direct[which, at_rows(c, q), :],
                wave * cap_rows * direct[which, at_rows(c, (q + 2) % 4), :],
                ring_recv[which, 0, index : index + 1, :] * has_above,
                ring_recv[which, 1, index : index + 1, :] * has_below,
                shift_rows,
            )

    def finish_image(which, half):
        shared(lg, (which, half)).wait_recv()
        for c, q in fields:
            rows = at_rows(c, q, half)
            value = images[which, rows, :] + lg_recv[which, half, spread(c, q), :]
            if which > 0:
                value = value - images[which - 1, rows, :]
            images[which, rows, :] = value

    def send_direction(which, half):
        for c in range(chunks):
            for kk in range(2):
                real, imag = complex_product(
                    images[which - 1, at_rows(c, kk, half), :],
                    images[which - 1, at_rows(c, 2 + kk, half), :],
                    weights[c, kk],
                )
                for q, value in ((kk, real), (2 + kk, imag)):
                    direct[which, at_rows(c, q, half), :] = value
                    tg_send[which - 1, half, spread(c, q), :] = value
        share(tg, (which - 1, half))

    def inner(a, b, half):
        total = jnp.zeros((8, 128), F32)
        for c, q in fields:
            term = a(c, q, half) * b(c, q, half)
            for i in range(group // 8):
                total = total + term[i * 8 : (i + 1) * 8]
        return total

    def image_rows(which):
        return lambda c, q, half: images[which, at_rows(c, q, half), :]

    def start_part(c, q, half):
        return start_rows[c, q, half * group : (half + 1) * group, :]

    def closed(total):
        return jnp.sum(jnp.sum(total, axis=0, keepdims=True), axis=1, keepdims=True)

    for half in range(2):
        shared(zf, (half,)).wait_recv()
        for c, q in fields:
            direct[0, at_rows(c, q, half), :] = zf_recv[half, spread(c, q), :]
    send_ring(0)
    for d in range(1, chunks):
        start_copy(d).start()
    receive(3)
    receive(4)
    local_image(0)

    dots = {}
    for which in (1, 2):
        for half in range(2):
            finish_image(which - 1, half)
            send_direction(which, half)
        send_ring(which)
        for d in range(1, chunks):
            back_copy(which, d).start()
        size = 4 * deep
        own = pl.ds(pl.multiple_of(zh * size, size), size)
        direct_back[which - 1, own, :] = direct[which, own, :]
        for half in range(2):
            shared(tg, (which - 1, half)).wait_recv()
            to_spec(slopes[half] * product(inv, tg_recv[which - 1, half]), which, half)
        local_image(which)
        if which == 1:
            for d in range(1, chunks):
                start_copy(d).wait_recv()
        now = image_rows(which - 1)
        for name, other in [("start", start_part)] + [(j, image_rows(j)) for j in range(which)]:
            dots[name, which - 1] = closed(inner(other, now, 0) + inner(other, now, 1))
    others = [("start", start_part)] + [(j, image_rows(j)) for j in range(3)]
    sums = []
    for half in range(2):
        finish_image(2, half)
        sums.append([inner(other, image_rows(2), half) for _, other in others])
    for (name, _), one, two in zip(others, *sums):
        dots[name, 2] = closed(one + two)

    names = list(dots)
    lane = lax.broadcasted_iota(jnp.int32, (1, 128), 1)
    packed = sum(jnp.where(lane == i, dots[name], 0.0) for i, name in enumerate(names))
    ar_send[...] = packed

    def push(other, _):
        copy(ar_send, ar_recv.at[harm], a_ssem.at[0], a_rsem.at[0], (other, node)).start()

    each_peer(push)
    ar_recv[harm] = packed
    all_sums = copy(
        ar_recv.at[pl.ds(0, 63)], ar_recv.at[pl.ds(0, 63)], a_ssem.at[0], a_rsem.at[0],
        (prev_harm, node),
    )
    for half in range(2):
        for stage in range(2):
            exchanged(ta, (stage, half)).wait_send()
            shared(tg, (stage, half)).wait_send()
        exchanged(la, (half,)).wait_send()
        shared(zf, (half,)).wait_send()
        for stage in range(3):
            shared(lg, (stage, half)).wait_send()
    for side in range(2):
        halo_copy(side).wait_send()
        for stage in range(3):
            ring_copy(stage, side).wait_send()
    for d in range(1, chunks):
        start_copy(d).wait_send()
        for which in (1, 2):
            back_copy(which, d).wait_send()
    for way, at in moves:
        along_z(way, at).wait_send()
        for dx in (1, 2, 3):
            along_x(way, at, dx).wait_send()
    all_sums.wait_recv()
    total = jnp.sum(ar_recv[...], axis=0)
    ax_send[...] = total

    def ax_copy(dx):
        return copy(
            ax_send, ax_recv.at[node], x_ssem.at[dx - 1], x_rsem.at[dx - 1],
            (harm, lax.rem(node + dx, 4)),
        )

    for dx in (1, 2, 3):
        ax_copy(dx).start()
    ax_recv[node] = total
    for which in (1, 2):
        for d in range(1, chunks):
            back_copy(which, d).wait_recv()
    for dx in (1, 2, 3):
        ax_copy(dx).wait_recv()
    total = jnp.sum(ax_recv[...], axis=0)
    value = {name: total[:, i : i + 1] for i, name in enumerate(names)}

    g00, g01, g02 = value[0, 0], value[0, 1], value[0, 2]
    g11, g12, g22 = value[1, 1], value[1, 2], value[2, 2]
    b0, b1, b2 = value["start", 0], value["start", 1], value["start", 2]
    l10, l20 = g01 / g00, g02 / g00
    d1 = g11 - l10 * g01
    e12 = g12 - l10 * g02
    c1 = b1 - l10 * b0
    l21 = e12 / d1
    d2 = g22 - l20 * g02 - l21 * e12
    c2 = b2 - l20 * b0 - l21 * c1
    y2 = c2 / d2
    y1 = (c1 - e12 * y2) / d1
    y0 = (b0 - g01 * y1 - g02 * y2) / g00
    w0, w1, w2 = y0 - y1 + y2, y1 - y2, y2
    outs = [resid_out]
    for p, kk in pairs:
        q = p * 2 + kk
        for c in range(chunks):
            rows = slice(c * deep, (c + 1) * deep)
            out_update[p, kk, rows, :] = (
                w0 * first_z[q, rows, :]
                + w1 * direct_back[0, at_rows(c, q), :]
                + w2 * direct_back[1, at_rows(c, q), :]
            )
        outs.append(
            pltpu.make_async_copy(out_update.at[p, kk], update_hbm.at[p, kk], out_sem.at[q])
        )
        outs[-1].start()

    all_sums.wait_send()
    for dx in (1, 2, 3):
        ax_copy(dx).wait_send()
    for out in outs:
        out.wait()


def body(state, source, capacity, row_shift, device_type, device_table, precond):
    inverse, forward = tables(state.shape[1] * lax.axis_size("harm"))
    block = (2, 2, 128, 128)
    chunks, group = 8 // FOLD, 8 * FOLD
    vmem = pltpu.VMEM
    dma = pltpu.SemaphoreType.DMA
    hbm = pl.BlockSpec(memory_space=pltpu.HBM)

    def four(*lead):
        return [vmem(lead + (256, 128), F32)] * 2

    update, resid = pl.pallas_call(
        kernel,
        out_shape=[jax.ShapeDtypeStruct(block, F32)] * 2,
        in_specs=[hbm] * 5 + [pl.BlockSpec(memory_space=pltpu.SMEM)] + [hbm] * 3,
        out_specs=[hbm] * 2,
        scratch_shapes=[
            vmem(block, F32), vmem(block, F32), vmem((128, 128), F32), vmem((1, 128), jnp.int32),
            vmem((128, 128), jnp.int32), vmem(block, F32), vmem((512, 256), BF16),
            vmem((512, 256), BF16),
            vmem((chunks, 2, 128, 256), F32), vmem((chunks, 2, 256, 256), BF16),
            vmem((2, 256, 128), F32), vmem((128, 128), F32), vmem((4, 128, 128), F32),
            vmem((chunks, 4, 2 * group, 128), F32), vmem((4, 128, 128), F32),
            vmem((3, 512, 128), F32), vmem((3, 512, 128), F32), vmem((2, 512, 128), F32),
            vmem(block, F32), vmem(block, F32),
            *four(2, 2), *four(2), vmem((2, 256, 128), F32), *four(3, 2), *four(2, 2),
            vmem((2, 8, 128), F32), vmem((2, 8, 128), F32),
            vmem((3, 2, 4 * chunks, 128), F32), vmem((3, 2, 4 * chunks, 128), F32),
            vmem((1, 128), F32), vmem((64, 1, 128), F32),
            vmem((1, 128), F32), vmem((4, 1, 128), F32),
            dma((8,)), dma((5,)), dma((2, 2)), dma((2, 2)), dma((2,)), dma((2,)), dma((2,)), dma((2,)),
            dma((3, 2)), dma((3, 2)), dma((2, 2)), dma((2, 2)), dma((2,)), dma((2,)),
            dma((3, 2)), dma((3, 2)), dma((chunks - 1,)), dma((chunks - 1,)),
            dma((chunks - 1, 3)), dma((chunks - 1, 3)), dma((3, chunks - 1)),
            dma((3, chunks - 1)), dma((1,)), dma((1,)), dma((3,)), dma((3,)),
        ],
        compiler_params=pltpu.CompilerParams(
            collective_id=0, has_side_effects=True, vmem_limit_bytes=67_000_000
        ),
    )(
        state, source, capacity, row_shift.reshape(1, -1), device_type, device_table, precond,
        jnp.asarray(inverse), jnp.asarray(forward),
    )
    return update, resid


def solution(mesh):
    harm, node = mesh.axis_names
    return jax.shard_map(
        body,
        mesh=mesh,
        in_specs=(
            P(None, harm, node, None),
            P(None, harm, node, None),
            P(node, None),
            P(node),
            P(node, None),
            P(),
            P(None, harm, None, None),
        ),
        out_specs=(P(None, harm, node, None), P(None, harm, node, None)),
        check_vma=False,
    )
```

time: 87.8 us -> 81.9 us (0.933)
  Pallas kernels: 84.6 us -> 78.7 us
    pallas_call x1, Pallas kernels: 84.6 us -> 78.7 us  [body(): pl.pallas_call(kernel, out_shape=[jax.ShapeDtypeStruct(block, F32)] * 2,...]
where the time goes in v3:
time: 81.9 us; the launch traced here: 81.8 us
  Pallas kernels  78.7 us (96%)
  local copies, waits for them, and re-layouts  2.42 us (3%)
    pallas_call x1, Pallas kernels, body(): pl.pallas_call(kernel, out_shape=[jax.ShapeDtypeStruct(block, F32)] * 2,...  78.7 us
    unnamed x4, local copies, waits for them, and re-layouts  2.42 us

profile of v3, /device:TPU:1, one launch (start us, length us, event | category | flops | bytes accessed | tf_op | source)
XLA Modules:
  0.0 81.8 jit_solution(5617757452392922857)
XLA Ops:
  0.6 78.7 %shard_map.104 = (f32[2,2,128,128]{3,2,1,0:T(8,128)}, f32[2,2,128,128]{3,2,1,0:T(8,128)}) custom-call(f32[2,2,128,128]{3,2,1,0:T(8,128)} %state_hbm.1, f32[2,2,128,128]{3,2,1,0:T(8,128)} %source_hbm.1, f32[128,128]{1,0:T(8,128)} %cap_hbm.1, s32[1,128]{1,0:T(1,128)} %bitcast.1, s32[128,128]{1,0:T(8,128)} %kinds_hbm.1, f32[3,4]{1,0:T(4,128)} %table.1, ...), custom_call_target="tpu_custom_call" | custom-call | tf_op jit(solution)/shard_map/pallas_call | solution.py:629
  79.3 0.0 copy-start
  79.3 1.7 %copy.13 = f32[2,2,128,128]{3,2,1,0:T(8,128)} copy(f32[2,2,128,128]{3,2,1,0:T(8,128)} %get-tuple-element.4) | data formatting | bytes 524288
  81.0 0.0 copy-done
  81.0 0.7 copy.14
Async XLA Ops:
  79.3 1.7 %copy-start = (f32[2,2,128,128]{3,2,1,0:T(8,128)S(1)}, f32[2,2,128,128]{3,2,1,0:T(8,128)}, u32[]{:S(2)}) copy-start(f32[2,2,128,128]{3,2,1,0:T(8,128)} %get-tuple-element.5) | copy-start | bytes 786436

commit v4 on v3

--- a/solution.py
+++ b/solution.py
@@ -142,7 +142,7 @@
         def push(other, other_slot):
             copy(
                 send.at[*at, unit(other_slot)], recv.at[*at, unit(slot)],
-                ssem.at[*at], rsem.at[*at], (other, node),
+                ssem.at[0], rsem.at[*at], (other, node),
             ).start()
 
         each_peer(push)
@@ -152,7 +152,7 @@
         send, recv, ssem, rsem = bufs
         rows = pl.ds(0, 252)
         return copy(
-            send.at[*at, rows], recv.at[*at, rows], ssem.at[*at], rsem.at[*at], (prev_harm, node)
+            send.at[*at, rows], recv.at[*at, rows], ssem.at[0], rsem.at[*at], (prev_harm, node)
         )
 
     wide = 4 * chunks
@@ -164,7 +164,7 @@
         def push(other, place):
             copy(
                 send.at[*at, pl.ds(pl.multiple_of(place * wide, wide), wide)], recv.at[*at, own],
-                ssem.at[*at], rsem.at[*at], (other, node),
+                ssem.at[0], rsem.at[*at], (other, node),
             ).start()
 
         each_mate(push)
@@ -175,7 +175,7 @@
         rows = pl.ds(0, 256 - wide)
         return copy(
             send.at[*at, rows], recv.at[*at, rows],
-            ssem.at[*at], rsem.at[*at], (prev_harm, node),
+            ssem.at[0], rsem.at[*at], (prev_harm, node),
         )
 
     def spread(c, q):
@@ -190,14 +190,21 @@
     def halo_copy(side):
         step = 1 if side == 0 else 3
         return copy(
-            halo_send.at[side], halo_recv.at[side], h_ssem.at[side], h_rsem.at[side],
+            halo_send.at[side], halo_recv.at[side], h_ssem.at[0], h_rsem.at[0],
             (harm, lax.rem(node + step, 4)),
         )
 
+    halo_both = copy(halo_send, halo_recv, h_ssem.at[0], h_rsem.at[0], ring[0])
+
     def ring_copy(stage, side):
         return copy(
             ring_send.at[stage, side], ring_recv.at[stage, side],
-            r_ssem.at[stage, side], r_rsem.at[stage, side], ring[side],
+            r_ssem.at[0], r_rsem.at[stage], ring[side],
+        )
+
+    def ring_both(stage):
+        return copy(
+            ring_send.at[stage], ring_recv.at[stage], r_ssem.at[0], r_rsem.at[stage], ring[0]
         )
 
     pairs = [(p, kk) for p in range(2) for kk in range(2)]
@@ -261,25 +268,25 @@
     def along_z(way, step):
         high = along(step - 1 if way else chunks - (step - 1) if step > 1 else 0)[1]
         place = gathered.at[high, :, quarter]
-        index = 4 * way + step - 1
         target = along(chunks - 1 if way else 1)[0]
-        return copy(place, place, gz_ssem.at[index], gz_rsem.at[index], (target, node))
+        return copy(place, place, gz_ssem.at[0], gz_rsem.at[step - 1], (target, node))
 
     def along_x(way, step, dx):
         high = along(step if way else chunks - step)[1]
         place = gathered.at[high, :, quarter]
-        index = 4 * way + step - 1
-        return copy(
-            place, place, gx_ssem.at[index, dx - 1], gx_rsem.at[index, dx - 1],
-            (harm, lax.rem(node + dx, 4)),
-        )
+        return copy(
+            place, place, gx_ssem.at[0], gx_rsem.at[step - 1], (harm, lax.rem(node + dx, 4))
+        )
+
+    def bulk(count, rows, ssem, rsem):
+        place = gathered.at[pl.ds(0, count), :, pl.ds(0, rows)]
+        return copy(place, place, ssem, rsem, (prev_harm, node))
 
     moves = [(way, step) for step in (1, 2, 3, 4) for way in (0, 1) if way == 0 or step < 4]
 
     def pass_on(step):
-        for way, at in moves:
-            if at == step:
-                along_z(way, at).wait_recv()
+        ways = 2 if step < 4 else 1
+        bulk(ways, 32, gz_ssem.at[0], gz_rsem.at[step - 1]).wait_recv()
         for way, at in moves:
             if at == step + 1:
                 along_z(way, at).start()
@@ -289,10 +296,10 @@
                     along_x(way, at, dx).start()
 
     def receive(step):
+        ways = 2 if step < 4 else 1
+        bulk(ways, 96, gx_ssem.at[0], gx_rsem.at[step - 1]).wait_recv()
         for way, at in moves:
             if at == step:
-                for dx in (1, 2, 3):
-                    along_x(way, at, dx).wait_recv()
                 build(along(at if way else chunks - at)[1])
 
     for way, at in moves:
@@ -340,8 +347,7 @@
         exchange(la, (half,))
 
     evaluate(0)
-    for side in range(2):
-        halo_copy(side).wait_recv()
+    halo_both.wait_recv()
     not_first = jnp.where(node == 0, 0.0, 1.0)
     not_last = jnp.where(node == 3, 0.0, 1.0)
     for p, kk in pairs:
@@ -379,7 +385,7 @@
     receive(1)
     for p, kk in pairs:
         out_resid[p, kk] = -start[p * 2 + kk]
-    resid_out = pltpu.make_async_copy(out_resid, resid_hbm, out_sem.at[4])
+    resid_out = pltpu.make_async_copy(out_resid, resid_hbm, out_sem.at[1])
     resid_out.start()
     def to_spec(signal, stage, half):
         lg_send[stage, half] = product(fwd, signal)
@@ -396,7 +402,7 @@
         other, high = along(d)
         return copy(
             start.at[:, pl.ds(pl.multiple_of(high * deep, deep), deep)], start_rows.at[zh],
-            b_ssem.at[0, d - 1], b_rsem.at[0, d - 1], (other, node),
+            b_ssem.at[0], b_rsem.at[0], (other, node),
         )
 
     def back_copy(which, d):
@@ -405,10 +411,19 @@
         return copy(
             direct.at[which, pl.ds(pl.multiple_of(high * size, size), size)],
             direct_back.at[which - 1, pl.ds(pl.multiple_of(zh * size, size), size)],
-            b_ssem.at[which, d - 1], b_rsem.at[which, d - 1], (other, node),
+            b_ssem.at[1], b_rsem.at[1], (other, node),
         )
 
     start_rows[zh] = start[:, pl.ds(pl.multiple_of(zh * deep, deep), deep), :]
+
+    rows_of_others = start_rows.at[pl.ds(0, chunks - 1)]
+    start_all = copy(
+        rows_of_others, rows_of_others, b_ssem.at[0], b_rsem.at[0], (prev_harm, node)
+    )
+    back_of_others = direct_back.at[:, pl.ds(0, 512 - 4 * deep)]
+    back_all = copy(
+        back_of_others, back_of_others, b_ssem.at[1], b_rsem.at[1], (prev_harm, node)
+    )
 
     fields = [(c, q) for c in range(chunks) for q in range(4)]
 
@@ -429,8 +444,7 @@
     has_below = jnp.where((node == 3) & (zh == chunks - 1), 0.0, 1.0)
 
     def local_image(which):
-        for side in range(2):
-            ring_copy(which, side).wait_recv()
+        ring_both(which).wait_recv()
         cap_rows, shift_rows = cap[chunk, :], shifts[chunk, :]
         for c, q in fields:
             p, kk = q // 2, q % 2
@@ -511,8 +525,7 @@
             to_spec(slopes[half] * product(inv, tg_recv[which - 1, half]), which, half)
         local_image(which)
         if which == 1:
-            for d in range(1, chunks):
-                start_copy(d).wait_recv()
+            start_all.wait_recv()
         now = image_rows(which - 1)
         for name, other in [("start", start_part)] + [(j, image_rows(j)) for j in range(which)]:
             dots[name, which - 1] = closed(inner(other, now, 0) + inner(other, now, 1))
@@ -538,44 +551,38 @@
         ar_recv.at[pl.ds(0, 63)], ar_recv.at[pl.ds(0, 63)], a_ssem.at[0], a_rsem.at[0],
         (prev_harm, node),
     )
-    for half in range(2):
-        for stage in range(2):
-            exchanged(ta, (stage, half)).wait_send()
-            shared(tg, (stage, half)).wait_send()
-        exchanged(la, (half,)).wait_send()
-        shared(zf, (half,)).wait_send()
-        for stage in range(3):
-            shared(lg, (stage, half)).wait_send()
-    for side in range(2):
-        halo_copy(side).wait_send()
-        for stage in range(3):
-            ring_copy(stage, side).wait_send()
-    for d in range(1, chunks):
-        start_copy(d).wait_send()
-        for which in (1, 2):
-            back_copy(which, d).wait_send()
-    for way, at in moves:
-        along_z(way, at).wait_send()
-        for dx in (1, 2, 3):
-            along_x(way, at, dx).wait_send()
+    def left(part, ssem):
+        copy(part, part, ssem, a_rsem.at[0], (prev_harm, node)).wait_send()
+
+    left(ta_send.at[:, :, pl.ds(0, 252)], ta_ssem.at[0])
+    left(la_send.at[:, pl.ds(0, 252)], la_ssem.at[0])
+    left(zf_recv.at[:, pl.ds(0, 256 - wide)], zf_ssem.at[0])
+    left(lg_send.at[:, :, pl.ds(0, 256 - wide)], lg_ssem.at[0])
+    left(tg_send.at[:, :, pl.ds(0, 256 - wide)], tg_ssem.at[0])
+    left(ring_send, r_ssem.at[0])
+    halo_both.wait_send()
+    bulk(7, 32, gz_ssem.at[0], gz_rsem.at[0]).wait_send()
+    bulk(7, 96, gx_ssem.at[0], gx_rsem.at[0]).wait_send()
+    start_all.wait_send()
+    back_all.wait_send()
     all_sums.wait_recv()
     total = jnp.sum(ar_recv[...], axis=0)
     ax_send[...] = total
 
     def ax_copy(dx):
         return copy(
-            ax_send, ax_recv.at[node], x_ssem.at[dx - 1], x_rsem.at[dx - 1],
+            ax_send, ax_recv.at[node], x_ssem.at[0], x_rsem.at[0],
             (harm, lax.rem(node + dx, 4)),
         )
 
     for dx in (1, 2, 3):
         ax_copy(dx).start()
     ax_recv[node] = total
-    for which in (1, 2):
-        for d in range(1, chunks):
-            back_copy(which, d).wait_recv()
-    for dx in (1, 2, 3):
-        ax_copy(dx).wait_recv()
+    back_all.wait_recv()
+    ax_all = copy(
+        ax_recv.at[pl.ds(0, 3)], ax_recv.at[pl.ds(0, 3)], x_ssem.at[0], x_rsem.at[0], ring[0]
+    )
+    ax_all.wait_recv()
     total = jnp.sum(ax_recv[...], axis=0)
     value = {name: total[:, i : i + 1] for i, name in enumerate(names)}
 
@@ -593,7 +600,6 @@
     y1 = (c1 - e12 * y2) / d1
     y0 = (b0 - g01 * y1 - g02 * y2) / g00
     w0, w1, w2 = y0 - y1 + y2, y1 - y2, y2
-    outs = [resid_out]
     for p, kk in pairs:
         q = p * 2 + kk
         for c in range(chunks):
@@ -603,16 +609,25 @@
                 + w1 * direct_back[0, at_rows(c, q), :]
                 + w2 * direct_back[1, at_rows(c, q), :]
             )
-        outs.append(
-            pltpu.make_async_copy(out_update.at[p, kk], update_hbm.at[p, kk], out_sem.at[q])
-        )
-        outs[-1].start()
+        pltpu.make_async_copy(out_update.at[p, kk], update_hbm.at[p, kk], out_sem.at[0]).start()
 
     all_sums.wait_send()
-    for dx in (1, 2, 3):
-        ax_copy(dx).wait_send()
-    for out in outs:
-        out.wait()
+    ax_all.wait_send()
+    pltpu.make_async_copy(out_update, update_hbm, out_sem.at[0]).wait()
+    resid_out.wait()
+
+
+def hand_over(update, resid, update_out, resid_out, held, in_sem, out_sem):
+    ways = [(update, update_out), (resid, resid_out)]
+    loads = [pltpu.make_async_copy(a, held.at[i], in_sem.at[i]) for i, (a, _) in enumerate(ways)]
+    stores = [pltpu.make_async_copy(held.at[i], b, out_sem.at[i]) for i, (_, b) in enumerate(ways)]
+    for load in loads:
+        load.start()
+    for load, store in zip(loads, stores):
+        load.wait()
+        store.start()
+    for store in stores:
+        store.wait()
 
 
 def body(state, source, capacity, row_shift, device_type, device_table, precond):
@@ -645,11 +660,10 @@
             vmem((3, 2, 4 * chunks, 128), F32), vmem((3, 2, 4 * chunks, 128), F32),
             vmem((1, 128), F32), vmem((64, 1, 128), F32),
             vmem((1, 128), F32), vmem((4, 1, 128), F32),
-            dma((8,)), dma((5,)), dma((2, 2)), dma((2, 2)), dma((2,)), dma((2,)), dma((2,)), dma((2,)),
-            dma((3, 2)), dma((3, 2)), dma((2, 2)), dma((2, 2)), dma((2,)), dma((2,)),
-            dma((3, 2)), dma((3, 2)), dma((chunks - 1,)), dma((chunks - 1,)),
-            dma((chunks - 1, 3)), dma((chunks - 1, 3)), dma((3, chunks - 1)),
-            dma((3, chunks - 1)), dma((1,)), dma((1,)), dma((3,)), dma((3,)),
+            dma((8,)), dma((2,)), dma((1,)), dma((2, 2)), dma((1,)), dma((2,)), dma((1,)),
+            dma((2,)), dma((1,)), dma((3, 2)), dma((1,)), dma((2, 2)), dma((1,)), dma((1,)),
+            dma((1,)), dma((3,)), dma((1,)), dma((4,)), dma((1,)), dma((4,)), dma((2,)),
+            dma((2,)), dma((1,)), dma((1,)), dma((1,)), dma((1,)),
         ],
         compiler_params=pltpu.CompilerParams(
             collective_id=0, has_side_effects=True, vmem_limit_bytes=67_000_000
@@ -658,7 +672,14 @@
         state, source, capacity, row_shift.reshape(1, -1), device_type, device_table, precond,
         jnp.asarray(inverse), jnp.asarray(forward),
     )
-    return update, resid
+    return pl.pallas_call(
+        hand_over,
+        out_shape=[jax.ShapeDtypeStruct(block, F32)] * 2,
+        in_specs=[hbm] * 2,
+        out_specs=[hbm] * 2,
+        scratch_shapes=[vmem((2,) + block, F32), dma((2,)), dma((2,))],
+        compiler_params=pltpu.CompilerParams(vmem_limit_bytes=67_000_000),
+    )(update, resid)
 
 
 def solution(mesh):

time: 81.9 us -> 80.2 us (0.979)
  local copies, waits for them, and re-layouts: 2.42 us -> 0 us
    unnamed x4 -> x0, local copies, waits for them, and re-layouts: 2.42 us -> none
    pallas_call x0 -> x1, Pallas kernels: none -> 1.77 us  [body(): pl.pallas_call(hand_over, out_shape=[jax.ShapeDtypeStruct(block, F32)] *...]
    pallas_call x1, Pallas kernels: 78.7 us -> 77.7 us  [body(): pl.pallas_call(kernel, out_shape=[jax.ShapeDtypeStruct(block, F32)] * 2,...]
where the time goes in v4:
time: 80.2 us; the launch traced here: 80.1 us
  Pallas kernels  79.4 us (99%)
    pallas_call x1, Pallas kernels, body(): pl.pallas_call(kernel, out_shape=[jax.ShapeDtypeStruct(block, F32)] * 2,...  77.7 us
    pallas_call x1, Pallas kernels, body(): pl.pallas_call(hand_over, out_shape=[jax.ShapeDtypeStruct(block, F32)] *...  1.77 us

profile of v4, /device:TPU:1, one launch (start us, length us, event | category | flops | bytes accessed | tf_op | source)
XLA Modules:
  0.0 80.1 jit_solution(4265176876558332512)
XLA Ops:
  0.6 77.7 %shard_map.104 = (f32[2,2,128,128]{3,2,1,0:T(8,128)}, f32[2,2,128,128]{3,2,1,0:T(8,128)}) custom-call(f32[2,2,128,128]{3,2,1,0:T(8,128)} %state_hbm.1, f32[2,2,128,128]{3,2,1,0:T(8,128)} %source_hbm.1, f32[128,128]{1,0:T(8,128)} %cap_hbm.1, s32[1,128]{1,0:T(1,128)} %bitcast.1, s32[128,128]{1,0:T(8,128)} %kinds_hbm.1, f32[3,4]{1,0:T(4,128)} %table.1, ...), custom_call_target="tpu_custom_call" | custom-call | tf_op jit(solution)/shard_map/pallas_call | solution.py:644
  78.3 1.8 %shard_map.105 = (f32[2,2,128,128]{3,2,1,0:T(8,128)}, f32[2,2,128,128]{3,2,1,0:T(8,128)}) custom-call(f32[2,2,128,128]{3,2,1,0:T(8,128)} %get-tuple-element.4.update, f32[2,2,128,128]{3,2,1,0:T(8,128)} %get-tuple-element.5.resid), custom_call_target="tpu_custom_call" | custom-call | tf_op jit(solution)/shard_map/pallas_call | solution.py:675

commit v5 on v4

--- a/solution.py
+++ b/solution.py
@@ -126,6 +126,18 @@
         )
     for place in ring:
         pl.semaphore_signal(barrier, inc=1, device_id=place, device_id_type=MESH)
+    is_last, is_first = mine == group - 1, mine == 0
+
+    @pl.when(zh == 0)
+    def _():
+        place = (48 + (chunks - 1) * 2 + 1, prev_node)
+        pl.semaphore_signal(barrier, inc=1, device_id=place, device_id_type=MESH)
+
+    @pl.when(zh == chunks - 1)
+    def _():
+        pl.semaphore_signal(barrier, inc=1, device_id=(0, next_node), device_id_type=MESH)
+
+    greeters = 68 + jnp.where(is_last & (zh == chunks - 1) | is_first & (zh == 0), group, 0)
 
     def copy(src, dst, ssem, rsem, place):
         return pltpu.make_async_remote_copy(
@@ -201,6 +213,15 @@
             ring_send.at[stage, side], ring_recv.at[stage, side],
             r_ssem.at[0], r_rsem.at[stage], ring[side],
         )
+
+    def edge_rows(side):
+        high = lax.rem(zh + (1 if side == 0 else chunks - 1), chunks)
+        beside = next_node if side == 0 else prev_node
+        for place in range(group):
+            copy(
+                ta_recv.at[1, 1 - side, pl.ds(place * wide, wide)], ring_recv.at[0, side],
+                r_ssem.at[1], r_rsem.at[0], (place // 2 * 16 + high * 2 + place % 2, beside),
+            ).start()
 
     def ring_both(stage):
         return copy(
@@ -252,7 +273,7 @@
         )
     shifts[...] = jnp.broadcast_to(shift[...].astype(F32), (128, 128)).T
 
-    pl.semaphore_wait(barrier, 68)
+    pl.semaphore_wait(barrier, greeters)
     exchange(ta, (0, 0))
     to_time(state, 0, 1)
     exchange(ta, (0, 1))
@@ -290,10 +311,17 @@
         for way, at in moves:
             if at == step + 1:
                 along_z(way, at).start()
-        for dx in (2, 1, 3):
+        for dx in (2, 1, 3) if step != 3 else (1, 3):
             for way, at in moves:
                 if at == step:
                     along_x(way, at, dx).start()
+
+    def pass_rest():
+        rows = pl.ds(pl.multiple_of(lax.rem(node + 2, 4) * 32, 32), 32)
+        for way in (0, 1):
+            place = gathered.at[along(2 if way else chunks - 2)[1], :, rows]
+            target = along(chunks - 1 if way else 1)[0]
+            copy(place, place, gx_ssem.at[0], gx_rsem.at[2], (target, node)).start()
 
     def receive(step):
         ways = 2 if step < 4 else 1
@@ -394,9 +422,11 @@
     for half in range(2):
         exchanged(ta, (1, half)).wait_recv()
         share(zf, (half,))
+        pl.when(is_last if half else is_first)(functools.partial(edge_rows, 1 - half))
         to_spec(slopes[half] * product(inv, ta_recv[1, half]), 0, half)
         pass_on(3 + half)
     receive(2)
+    pass_rest()
 
     def start_copy(d):
         other, high = along(d)
@@ -502,7 +532,6 @@
         shared(zf, (half,)).wait_recv()
         for c, q in fields:
             direct[0, at_rows(c, q, half), :] = zf_recv[half, spread(c, q), :]
-    send_ring(0)
     for d in range(1, chunks):
         start_copy(d).start()
     receive(3)
@@ -559,7 +588,12 @@
     left(zf_recv.at[:, pl.ds(0, 256 - wide)], zf_ssem.at[0])
     left(lg_send.at[:, :, pl.ds(0, 256 - wide)], lg_ssem.at[0])
     left(tg_send.at[:, :, pl.ds(0, 256 - wide)], tg_ssem.at[0])
-    left(ring_send, r_ssem.at[0])
+    left(ring_send.at[pl.ds(1, 2)], r_ssem.at[0])
+
+    @pl.when(is_last | is_first)
+    def _():
+        left(ta_recv.at[1, 0], r_ssem.at[1])
+
     halo_both.wait_send()
     bulk(7, 32, gz_ssem.at[0], gz_rsem.at[0]).wait_send()
     bulk(7, 96, gx_ssem.at[0], gx_rsem.at[0]).wait_send()
@@ -662,7 +696,7 @@
             vmem((1, 128), F32), vmem((4, 1, 128), F32),
             dma((8,)), dma((2,)), dma((1,)), dma((2, 2)), dma((1,)), dma((2,)), dma((1,)),
             dma((2,)), dma((1,)), dma((3, 2)), dma((1,)), dma((2, 2)), dma((1,)), dma((1,)),
-            dma((1,)), dma((3,)), dma((1,)), dma((4,)), dma((1,)), dma((4,)), dma((2,)),
+            dma((2,)), dma((3,)), dma((1,)), dma((4,)), dma((1,)), dma((4,)), dma((2,)),
             dma((2,)), dma((1,)), dma((1,)), dma((1,)), dma((1,)),
         ],
         compiler_params=pltpu.CompilerParams(

time: 80.2 us -> 77.1 us (0.961)
  Pallas kernels: 79.4 us -> 76.3 us
    pallas_call x1, Pallas kernels: 77.7 us -> 74.6 us  [body(): pl.pallas_call(kernel, out_shape=[jax.ShapeDtypeStruct(block, F32)] * 2,...]
where the time goes in v5:
time: 77.1 us; the launch traced here: 77 us
  Pallas kernels  76.3 us (99%)
    pallas_call x1, Pallas kernels, body(): pl.pallas_call(kernel, out_shape=[jax.ShapeDtypeStruct(block, F32)] * 2,...  74.6 us
    pallas_call x1, Pallas kernels, body(): pl.pallas_call(hand_over, out_shape=[jax.ShapeDtypeStruct(block, F32)] *...  1.77 us

profile of v5, /device:TPU:1, one launch (start us, length us, event | category | flops | bytes accessed | tf_op | source)
XLA Modules:
  0.0 77.0 jit_solution(12726790777039751338)
XLA Ops:
  0.6 74.6 %shard_map.104 = (f32[2,2,128,128]{3,2,1,0:T(8,128)}, f32[2,2,128,128]{3,2,1,0:T(8,128)}) custom-call(f32[2,2,128,128]{3,2,1,0:T(8,128)} %state_hbm.1, f32[2,2,128,128]{3,2,1,0:T(8,128)} %source_hbm.1, f32[128,128]{1,0:T(8,128)} %cap_hbm.1, s32[1,128]{1,0:T(1,128)} %bitcast.1, s32[128,128]{1,0:T(8,128)} %kinds_hbm.1, f32[3,4]{1,0:T(4,128)} %table.1, ...), custom_call_target="tpu_custom_call" | custom-call | tf_op jit(solution)/shard_map/pallas_call | solution.py:678
  75.2 1.8 %shard_map.105 = (f32[2,2,128,128]{3,2,1,0:T(8,128)}, f32[2,2,128,128]{3,2,1,0:T(8,128)}) custom-call(f32[2,2,128,128]{3,2,1,0:T(8,128)} %get-tuple-element.4.update, f32[2,2,128,128]{3,2,1,0:T(8,128)} %get-tuple-element.5.resid), custom_call_target="tpu_custom_call" | custom-call | tf_op jit(solution)/shard_map/pallas_call | solution.py:709
